TPU v7x, 256 devices: a 4x2x16 block of a 4x16x16 slice. The times are simulated.
256 devices in a mesh: groups: 2 (over y), ctx: 128 (over x, z, core).
Axes of the slice: x: 4, y: 2, z: 16, core: 2. Of those that a mesh axis runs over, the one named last changes fastest.
The devices are a block of a 4x16x16 slice.
Arguments:
- queries: bfloat16 [256, 8192], P(('groups', 'ctx')), parts along dimension 0, may hold values from -120 to 120
- fresh_keys: bfloat16 [256, 512], P(('groups', 'ctx')), parts along dimension 0, may hold values from -4 to 4
- fresh_values: bfloat16 [256, 512], P(('groups', 'ctx')), parts along dimension 0, may hold values from -4 to 4
- cache_keys: bfloat16 [262144, 512], P(('groups', 'ctx')), parts along dimension 0, may hold values from -4 to 4
- stored_values: bfloat16 [262144, 512], P(('groups', 'ctx')), parts along dimension 0, may hold values from -4 to 4
- cache_lengths: int32 [256], P(('groups', 'ctx')), parts along dimension 0, may hold values from 1 to 1024, as said below
- positions: int32 [256], P('groups'), parts along dimension 0, may hold values from 0 to 127, each once
Outputs:
- attended: bfloat16 [256, 8192], P(('groups', 'ctx')), parts along dimension 0
There are 2 independent parts, one for each index of `groups`. A program takes and returns all parts, laid end to end along the dimension named above; each array names one. Nothing has to cross between parts.
Inputs may be any that keep to these rules, and one draw needn't show every extreme that they name: `cache_lengths`: each entry lies between 1 and 1024, and one shard has all 1024 slots live.
All inputs are finite; a program needn't handle non-finite values.
Results may differ from a plain program's by a relative error of at most 0.003.
Values may be sent and summed in bfloat16 or wider, within the bound.
No kernel may reach another device: no remote copies, remote signals or barrier semaphores. Data moves between devices by JAX's collectives and lax.ppermute only.
A program may use at most 128 MiB of HBM per device.

v0:
```python
import jax
import jax.numpy as jnp
from jax import lax
from jax.sharding import Mesh
from jax.sharding import PartitionSpec as P

HEADS_PER_GROUP = 16
HEAD_WIDTH = 128
CTX = ("ctx_0", "ctx_1", "ctx_2")
GROUPS_CTX = ("groups", "ctx_0", "ctx_1", "ctx_2")


def laid_out(tiles, dim):
    tiles = jnp.moveaxis(tiles, 0, dim)
    lengths = tiles.shape
    return tiles.reshape(*lengths[:dim], lengths[dim] * lengths[dim + 1], *lengths[dim + 2 :])


def stacked_from(x, axes, sequence):
    tiles = x
    for k in sequence:
        tiles = lax.all_gather(tiles, axes[k])
    done = sequence[::-1]
    back = [done.index(k) for k in range(len(axes))]
    tiles = tiles.transpose(*back, *range(len(axes), tiles.ndim))
    return tiles.reshape(-1, *x.shape)


def whole_of(x, axes, sequence, dim):
    return laid_out(stacked_from(x, axes, sequence), dim)


def side_by_side(arrays, axis, split_dim, concat_dim, along):
    both = jnp.concatenate(arrays, axis=along)
    filled, at, outs = (
        lax.all_to_all(both, axis, split_axis=split_dim, concat_axis=concat_dim, tiled=True),
        0,
        [],
    )
    for a in arrays:
        outs.append(lax.slice_in_dim(filled, at, at + a.shape[along], axis=along))
        at += a.shape[along]
    return tuple(outs)


def body(queries, fresh_keys, fresh_values, cache_keys, stored_values, cache_lengths, positions):
    device_rank = lax.axis_index(CTX)
    new_rows = fresh_keys.shape[0]
    cache_rows = cache_keys.shape[0]
    head_size = HEAD_WIDTH
    group_size = HEADS_PER_GROUP
    kv_heads = fresh_keys.shape[1] // head_size
    query_heads = kv_heads * group_size
    all_keys = jnp.concatenate([cache_keys, fresh_keys], axis=0)
    all_values = jnp.concatenate([stored_values, fresh_values], axis=0)
    gathered = whole_of(queries, CTX, (0, 1, 2), 0)
    total_new = gathered.shape[0]
    key_order = lax.dynamic_slice_in_dim(positions, device_rank * new_rows, new_rows, 0)
    live = jnp.arange(cache_rows, dtype=jnp.int32) < cache_lengths[0]
    cache_seen = jnp.broadcast_to(live[None, :], (total_new, cache_rows))
    new_seen = key_order[None, :] <= positions[:, None]
    visible = jnp.concatenate([cache_seen, new_seen], axis=1)
    maxima_list = []
    totals_list = []
    sums_list = []
    for head_group in range(kv_heads):
        query_part = gathered[
            :, head_group * group_size * head_size : (head_group + 1) * group_size * head_size
        ].reshape(total_new, group_size, head_size)
        key_part = all_keys[:, head_group * head_size : (head_group + 1) * head_size]
        value_part = all_values[:, head_group * head_size : (head_group + 1) * head_size]
        scores = jnp.einsum(
            "ngd,kd->ngk", query_part, key_part, preferred_element_type=jnp.float32
        ) * head_size ** (-0.5)
        scores = jnp.where(visible[:, None, :], scores, -jnp.inf)
        maxima = jnp.max(scores, axis=-1)
        weights = jnp.exp(scores - maxima[..., None]).astype(jnp.bfloat16)
        totals = jnp.sum(weights.astype(jnp.float32), axis=-1)
        sums = jnp.einsum("ngk,kd->ngd", weights, value_part, preferred_element_type=jnp.float32)
        maxima_list.append(maxima)
        totals_list.append(totals)
        sums_list.append(sums.reshape(total_new, group_size * head_size))
    block_max = jnp.concatenate(maxima_list, axis=1)
    block_total = jnp.concatenate(totals_list, axis=1)
    block_sum = jnp.concatenate(sums_list, axis=1)
    sums_in, maxima_in, totals_in = side_by_side(
        (block_sum[None], block_max[None], block_total[None]), CTX, 1, 0, 2
    )
    overall = jnp.max(maxima_in, axis=0)
    scale = jnp.exp(maxima_in - overall[None])
    sources = sums_in.shape[0]
    numerator = jnp.sum(
        sums_in.reshape(sources, new_rows, query_heads, head_size) * scale[..., None], axis=0
    )
    denominator = jnp.sum(totals_in * scale, axis=0)
    result = numerator / denominator[..., None]
    return result.reshape(new_rows, query_heads * head_size).astype(jnp.bfloat16)


def solution(mesh):
    finer = Mesh(
        mesh.devices.reshape(mesh.shape["groups"], 4, 16, 2), ("groups", "ctx_0", "ctx_1", "ctx_2")
    )
    return jax.shard_map(
        body,
        mesh=finer,
        in_specs=(
            P(GROUPS_CTX, None),
            P(GROUPS_CTX, None),
            P(GROUPS_CTX, None),
            P(GROUPS_CTX, None),
            P(GROUPS_CTX, None),
            P(GROUPS_CTX),
            P("groups"),
        ),
        out_specs=P(GROUPS_CTX, None),
        check_vma=False,
    )
```

profile of v0, /device:TPU:33, one launch (start us, length us, event | category | flops | bytes accessed | tf_op | source)
XLA Modules:
  0.0 457.8 jit_solution(15774616918609195429)
XLA Ops:
  6.6 10.8 %all-gather.3 = bf16[4,1,8192]{2,1,0:T(2,128)(2,1)S(1)} all-gather(bf16[1,1,8192]{2,1,0:T(2,128)(2,1)} %bitcast.126), channel_id=2, replica_groups=mesh['groups'=2,'ctx_0'=4,'ctx_1'=16,'ctx_2'=2] {'ctx_0'}, dimensions={0}, use_global_device_ids=true | all-gather | bytes 81920 | tf_op jit(solution)/shard_map/all_gather | solution.py:22
  17.3 0.7 copy.59
  18.2 74.2 %all-gather.10.cloned.1.call-done = bf16[16,4,8192]{2,1,0:T(4,128)(2,1)} async-done(((bf16[1,4,8192]{2,1,0:T(4,128)(2,1)}), bf16[16,4,8192]{2,1,0:T(4,128)(2,1)}) %all-gather.10.cloned.1.call-update) | async-done | bytes 1048592 | tf_op jit(solution)/shard_map/all_gather | solution.py:22
  93.1 1.2 dynamic_slice.3
  94.4 1.3 constant_dynamic-update-slice_fusion.1
  95.6 0.7 constant_dynamic-update-slice_fusion
  96.3 1.3 constant_dynamic-update-slice_fusion.3
  98.3 1.0 copy-done.2
  99.3 1.3 compare_bitcast_fusion
  100.8 21.9 %all-gather.8.cloned.1.call-done = bf16[32,4,1,8192]{3,1,2,0:T(4,128)(2,1)} async-done(((bf16[16,4,1,8192]{3,1,2,0:T(4,128)(2,1)}), bf16[32,4,1,8192]{3,1,2,0:T(4,128)(2,1)}) %all-gather.8.cloned.1.call-update) | async-done | bytes 2097168 | tf_op jit(solution)/shard_map/all_gather | solution.py:22
  122.7 5.1 %copy.58 = bf16[2,16,4,1,8192]{4,0,1,2,3:T(2,128)(2,1)} copy(bf16[2,16,4,1,8192]{4,2,1,0,3:T(4,128)(2,1)} %bitcast.116) | data formatting | bytes 4194304 | tf_op jit(solution)/shard_map/all_gather | solution.py:22
  127.8 2.7 reshape_reshape.3
  130.5 1.4 fusion.22
  131.9 1.3 copy.39
  133.3 1.3 copy.43
  134.6 4.5 fusion.10
  139.1 4.5 fusion.6
  143.8 4.5 fusion.8
  148.6 14.0 %fusion = (f32[128,16]{0,1:T(8,128)S(1)}, f32[128,16]{0,1:T(8,128)S(1)}, f32[128,16]{0,1:T(8,128)S(1)}, f32[128,16]{0,1:T(8,128)S(1)}, f32[1025,128,16]{1,0,2:T(8,128)}) fusion(pred[128,1025]{0,1:T(8,128)(4,1)S(1)} %pad_add_fusion, f32[1025,128,16]{1,0,2:T(8,128)} %fusion.10, f32[1025,128,16]{1,0,2:T(8,128)} %fusion.8, f32[1025,128,16]{1,0,2:T(8,128)} %fusion.6, ...), kind=kOutput, calls=%fused_computation.12 | convolution fusion | flops 562577408 | bytes 34540544 | tf_op jit(solution)/shard_map/ngd,kd->ngk/dot_general | solution.py:72
  162.7 12.7 %convert_reduce_fusion.3 = (f32[128,16]{0,1:T(8,128)S(1)}, f32[128,16]{0,1:T(8,128)S(1)}, f32[128,16]{0,1:T(8,128)S(1)}, f32[128,16]{0,1:T(8,128)S(1)}) fusion(f32[128,16]{0,1:T(8,128)S(1)} %get-tuple-element.9, f32[1025,128,16]{1,0,2:T(8,128)} %get-tuple-element.19, pred[128,1025]{0,1:T(8,128)(4,1)S(1)} %pad_add_fusion, f32[128,16]{0,1:T(8,128)S(1)} %get-tuple-element.12, ...), kind=kLoop, calls=%fused_computation.7 | loop fusion | flops 50372608 | bytes 33783936 | tf_op jit(solution)/shard_map/reduce_sum | solution.py:78
  175.4 5.7 %fusion.11 = f32[128,16,128]{0,2,1:T(8,128)S(1)} fusion(bf16[1025,512]{1,0:T(8,128)(2,1)S(1)} %copy-done.3, f32[1025,128,16]{1,0,2:T(8,128)} %get-tuple-element.19, f32[128,16]{0,1:T(8,128)S(1)} %get-tuple-element.9, pred[128,1025]{0,1:T(8,128)(4,1)S(1)} %pad_add_fusion), kind=kOutput, calls=%fused_computation.34 | convolution fusion | flops 545792000 | bytes 9849856 | tf_op jit(solution)/shard_map/ngk,kd->ngd/dot_general | solution.py:79
  181.2 2.2 fusion.9
  183.4 3.2 fusion.7
  186.6 3.1 fusion.5
  190.7 1.6 copy.47
  192.2 2.6 copy.48
  194.8 1.5 pad_maximum_fusion
  196.4 5.2 %broadcast_in_dim.55 = f32[1,128,8192]{2,0,1:T(1,128)} reshape(f32[128,8192]{1,0:T(8,128)S(1)} %pad_maximum_fusion) | data formatting | bytes 8388608 | tf_op jit(solution)/shard_map/broadcast_in_dim | solution.py:87
  201.6 25.9 %concatenate.27 = f32[1,128,8320]{2,0,1:T(1,128)} concatenate(f32[1,128,8192]{2,0,1:T(1,128)} %broadcast_in_dim.55, f32[1,128,64]{2,0,1:T(1,128)S(1)} %copy.49, f32[1,128,64]{2,0,1:T(1,128)S(1)} %copy.50), dimensions={2} | concatenate | bytes 8519680 | tf_op jit(solution)/shard_map/concatenate | solution.py:34
  227.5 211.4 %all_to_all.12 = f32[1,128,8320]{2,0,1:T(1,128)S(1)} all-to-all(f32[1,128,8320]{2,0,1:T(1,128)} %concatenate.27), channel_id=1, replica_groups=mesh['groups'=2,'ctx_0'=4,'ctx_1'=16,'ctx_2'=2] {'ctx_0','ctx_1','ctx_2'}, dimensions={1} | all-to-all | bytes 8519680 | tf_op jit(solution)/shard_map/all_to_all | solution.py:36
  439.3 2.5 mul.59
  441.9 8.3 %fusion.4 = f32[8192]{0:T(1024)S(1)} fusion(f32[128,1,8192]{2,1,0:T(1,128)} %bitcast.110, f32[128,1,8320]{2,1,0:T(1,128)S(1)} %bitcast.109), kind=kLoop, calls=%fused_computation.18 | loop fusion | flops 2088960 | bytes 8421376 | tf_op jit(solution)/shard_map/reduce_sum | solution.py:92
  (48 shorter events, 3.6 us)
Async XLA Ops:
  6.5 85.8 %all-gather.10.cloned.1.call-start = ((), (), s32[]{:S(2)}) async-start(), calls=%async_computation.2 | async-start | bytes 1114112 | tf_op jit(solution)/shard_map/all_gather | solution.py:22
  18.1 104.6 %all-gather.8.cloned.1.call-start = ((), (), s32[]{:S(2)}) async-start(), calls=%async_computation.1 | async-start | bytes 3145728 | tf_op jit(solution)/shard_map/all_gather | solution.py:22
  98.3 1.0 copy-start.2
  139.1 4.5 copy-start.1
  143.6 4.8 %copy-start = (bf16[128,2048]{1,0:T(8,128)(2,1)S(1)}, bf16[128,2048]{1,0:T(8,128)(2,1)}, u32[]{:S(2)}) copy-start(bf16[128,2048]{1,0:T(8,128)(2,1)} %get-tuple-element.18) | copy-start | bytes 1572868
  148.3 14.3 %slice-start = ((s8[8454144]{0:T(1024)(128)(4,1)}), s8[65536]{0:T(1024)(128)(4,1)S(1)}, s32[]{:S(2)}) async-start(s8[8454144]{0:T(1024)(128)(4,1)} %bitcast.101), calls=%async_computation.3 | async-start | bytes 131072
  148.6 14.1 %slice-start.1 = ((s8[8454144]{0:T(1024)(128)(4,1)}), s8[4194304]{0:T(1024)(128)(4,1)S(1)}, s32[]{:S(2)}) async-start(s8[8454144]{0:T(1024)(128)(4,1)} %bitcast.101), calls=%async_computation.4 | async-start | bytes 8388608
  148.6 14.1 %slice-start.2 = ((s8[8454144]{0:T(1024)(128)(4,1)}), s8[4194304]{0:T(1024)(128)(4,1)S(1)}, s32[]{:S(2)}) async-start(s8[8454144]{0:T(1024)(128)(4,1)} %bitcast.101), calls=%async_computation.5 | async-start | bytes 8388608
  148.6 32.5 %slice-start.3 = ((s8[8454144]{0:T(1024)(128)(4,1)}), s8[4194304]{0:T(1024)(128)(4,1)S(1)}, s32[]{:S(2)}) async-start(s8[8454144]{0:T(1024)(128)(4,1)} %bitcast.103), calls=%async_computation.6 | async-start | bytes 8388608
  148.6 32.5 %slice-start.4 = ((s8[8454144]{0:T(1024)(128)(4,1)}), s8[65536]{0:T(1024)(128)(4,1)S(1)}, s32[]{:S(2)}) async-start(s8[8454144]{0:T(1024)(128)(4,1)} %bitcast.103), calls=%async_computation.7 | async-start | bytes 131072
  162.7 12.7 %copy-start.3 = (bf16[1025,512]{1,0:T(8,128)(2,1)S(1)}, bf16[1025,512]{1,0:T(8,128)(2,1)}, u32[]{:S(2)}) copy-start(bf16[1025,512]{1,0:T(8,128)(2,1)} %copy-done.2) | copy-start | bytes 3148804
  162.7 18.4 %slice-start.5 = ((s8[8454144]{0:T(1024)(128)(4,1)}), s8[4194304]{0:T(1024)(128)(4,1)S(1)}, s32[]{:S(2)}) async-start(s8[8454144]{0:T(1024)(128)(4,1)} %bitcast.103), calls=%async_computation.8 | async-start | bytes 8388608
  175.4 8.0 %slice-start.6 = ((s8[8454144]{0:T(1024)(128)(4,1)}), s8[4194304]{0:T(1024)(128)(4,1)S(1)}, s32[]{:S(2)}) async-start(s8[8454144]{0:T(1024)(128)(4,1)} %bitcast.105), calls=%async_computation.9 | async-start | bytes 8388608
  175.4 8.0 %slice-start.7 = ((s8[8454144]{0:T(1024)(128)(4,1)}), s8[4194304]{0:T(1024)(128)(4,1)S(1)}, s32[]{:S(2)}) async-start(s8[8454144]{0:T(1024)(128)(4,1)} %bitcast.105), calls=%async_computation.10 | async-start | bytes 8388608
  181.2 2.2 slice-start.8
Sparse Core Ops, SparseCore 0:
  18.2 74.1 all-gather.9
  94.2 28.4 all-gather.7
where the time goes:
time: 460 us; the launch traced here: 458 us
  blocking collectives  222 us (48%)
  waiting for transfers between devices  96.2 us (21%)
  local copies, waits for them, and re-layouts  58.1 us (13%)
  matrix products  41.7 us (9%)
  other arithmetic  25.1 us (5%)
  between operations  14.4 us (3%)
    all_to_all x1, blocking collectives, side_by_side(): lax.all_to_all(both, axis, split_axis=split_dim, concat_axis=concat_dim,...  211 us
    all_gather x2, waiting for transfers between devices, stacked_from(): tiles = lax.all_gather(tiles, axes[k])  96.1 us
    dot_general x4, matrix products, body(): jnp.einsum('ngd,kd->ngk', query_part, key_part, preferred_element_type=jn...  27.5 us
    concatenate x1, local copies, waits for them, and re-layouts, side_by_side(): both = jnp.concatenate(arrays, axis=along)  25.9 us
    dot_general x4, matrix products, body(): jnp.einsum('ngk,kd->ngd', weights, value_part, preferred_element_type=jnp...  14.3 us
    reduce_sum x1, other arithmetic, body(): totals = jnp.sum(weights.astype(jnp.float32), axis=-1)  12.7 us
    all_gather x1, blocking collectives, stacked_from(): tiles = lax.all_gather(tiles, axes[k])  10.8 us
  transfers between devices with their start and end apart: 2, of which 2 were waited for; matrix products, arithmetic and copies ran while one was open for 1% of the time, Pallas kernels for 0%

commit v1 on v0

v1 whole, which is shorter than its diff:
```python
import functools
import math

import jax
import jax.numpy as jnp
from jax import lax
from jax.experimental import pallas as pl
from jax.experimental.pallas import tpu as pltpu
from jax.sharding import Mesh
from jax.sharding import PartitionSpec as P

HEADS_PER_GROUP = 16
HEAD_WIDTH = 128
GROUPS_CTX = ("groups", "x", "z", "core")
NX, NZ = 4, 16
LOG2_SCALE = HEAD_WIDTH ** (-0.5) * math.log2(math.e)
STAT_ROWS = 8
LSE_STEPS = 2.0**18
FULL = 32767.0
F32, BF16, I16, I32 = jnp.float32, jnp.bfloat16, jnp.int16, jnp.int32
SWAP = [(0, 1), (1, 0)]


def dot_nt(a, b):
    return lax.dot_general(a, b, (((1,), (1,)), ((), ())), preferred_element_type=F32)


def dot_nn(a, b):
    return lax.dot_general(a, b, (((1,), (0,)), ((), ())), preferred_element_type=F32)


def diagonal(rows):
    row = lax.broadcasted_iota(jnp.int32, (rows, 128), 0)
    lane = lax.broadcasted_iota(jnp.int32, (rows, 128), 1)
    return lax.rem(lane, rows) == row


def attend_kernel(len_ref, q_ref, k_ref, v_ref, kn_ref, vn_ref, bias_ref, o_ref, s_scr, sn_scr, acc_scr, m_scr, st_scr):
    tokens, kv_heads, group = q_ref.shape[:3]
    rows = tokens * group
    slots = k_ref.shape[2]
    tile = chunk = 256
    chunks = o_ref.shape[0]
    per = rows // chunks

    @pl.loop(0, kv_heads)
    def head(kv):
        @pl.loop(0, 2)
        def block(blk):
            live = len_ref[blk]

            def variant(n):
                for r in range(0, rows, tile):
                    t0, t1 = r // group, (r + tile) // group
                    q = q_ref[t0:t1, kv].reshape(tile, HEAD_WIDTH)
                    bias = bias_ref[blk, t0:t1]
                    bias = jnp.broadcast_to(bias[:, None, :], (t1 - t0, group, 128)).reshape(tile, 128)
                    s_new = dot_nt(q, kn_ref[kv]) + bias
                    sn_scr[r : r + tile] = s_new
                    top = s_new
                    for c in range(0, n, chunk):
                        s = dot_nt(q, k_ref[blk, kv, c : c + chunk, :])
                        if c + chunk > (n // 2 if n > chunk else 0):
                            col = lax.broadcasted_iota(jnp.int32, (1, chunk), 1) + c
                            s = s + jnp.where(col < live, 0.0, -jnp.inf)
                        s_scr[r : r + tile, c : c + chunk] = s
                        for l in range(0, chunk, 128):
                            top = jnp.maximum(top, s[:, l : l + 128])
                    top = jnp.max(top, axis=1, keepdims=True)
                    acc = None
                    for c in range(0, n, chunk):
                        p = jnp.exp2((s_scr[r : r + tile, c : c + chunk] - top) * LOG2_SCALE).astype(BF16)
                        v = v_ref[blk, kv, c : c + chunk, :]
                        term = dot_nn(p, jnp.concatenate([v, jnp.ones_like(v)], axis=1))
                        acc = term if acc is None else acc + term
                    p = jnp.exp2((sn_scr[r : r + tile] - top) * LOG2_SCALE).astype(BF16)
                    v = vn_ref[kv]
                    acc = acc + dot_nn(p, jnp.concatenate([v, jnp.ones_like(v)], axis=1))
                    acc_scr[blk, r : r + tile, :] = acc
                    m_scr[blk, r : r + tile, :] = jnp.broadcast_to(top * LOG2_SCALE, (tile, 128))

            low = 0
            for n in (slots // 4, slots // 2, slots):
                pl.when(jnp.logical_and(live > low, live <= n))(functools.partial(variant, n))
                low = n

        m_a, m_b = m_scr[0], m_scr[1]
        top = jnp.maximum(m_a, m_b)
        w_a, w_b = jnp.exp2(m_a - top), jnp.exp2(m_b - top)
        total = acc_scr[0, :, HEAD_WIDTH:] * w_a + acc_scr[1, :, HEAD_WIDTH:] * w_b
        mean = (acc_scr[0, :, :HEAD_WIDTH] * w_a + acc_scr[1, :, :HEAD_WIDTH] * w_b) / total
        lse = top + jnp.log2(total)
        at = pl.multiple_of(kv * per, per)
        coded, exponent = encode(mean)
        o_ref[:, pl.ds(at, per), :] = coded.reshape(chunks, per, HEAD_WIDTH).astype(I16)
        pick = diagonal(per)[None]
        st_scr[0, kv] = jnp.sum(jnp.where(pick, lse.reshape(chunks, per, 128), 0.0), axis=1)
        spread = jnp.broadcast_to(exponent, (rows, 128)).reshape(chunks, per, 128)
        st_scr[1, kv] = jnp.sum(jnp.where(pick, spread, 0.0), axis=1)

    write_stats(o_ref, [st_scr[0, kv] for kv in range(kv_heads)], [st_scr[1, kv] for kv in range(kv_heads)])


def encode(mean):
    largest = jnp.max(jnp.abs(mean), axis=-1, keepdims=True)
    exponent = jnp.ceil(jnp.log2(jnp.maximum(largest, 1e-30)))
    return jnp.round(mean * (FULL * jnp.exp2(-exponent))).astype(I32), exponent


def write_stats(o_ref, lses, exponents):
    steps = [jnp.round(l * LSE_STEPS).astype(I32) for l in lses]
    terms = [lax.shift_right_arithmetic(t, jnp.full_like(t, 16)) for t in steps]
    terms += [(t & 0xFFFF) - 32768 for t in steps]
    terms += [e.astype(I32) for e in exponents]
    terms += [jnp.zeros_like(terms[0])] * (STAT_ROWS - len(terms))
    rows = o_ref.shape[1] - STAT_ROWS
    o_ref[:, rows:, :] = jnp.stack(terms, axis=1).astype(I16)


def read_stats(stats):
    stats = stats.astype(I32)
    steps = stats[:, 0:2] * 65536 + (stats[:, 2:4] + 32768)
    return steps.astype(F32) * (1.0 / LSE_STEPS), jnp.exp2(stats[:, 4:6].astype(F32)) * (1.0 / FULL)


def as_column(w, per):
    chunks = w.shape[0]
    spread = jnp.broadcast_to(w[:, :, None, :], (chunks, 2, per, 128))
    lane = lax.broadcasted_iota(jnp.int32, (per, 128), 1)
    row = lax.broadcasted_iota(jnp.int32, (per, 128), 0)
    column = jnp.sum(jnp.where((lane == row)[None, None], spread, 0.0), axis=3, keepdims=True)
    return column.reshape(chunks, 2 * per, 1)


def numbers(coded):
    return coded.astype(I32).astype(F32)


def merge_kernel(*refs):
    pieces, o_ref = refs[:-1], refs[-1]
    rows = o_ref.shape[1] - STAT_ROWS
    lses, scales = zip(*[read_stats(p[:, rows:, :]) for p in pieces])
    top = functools.reduce(jnp.maximum, lses)
    weights = [jnp.exp2(l - top) for l in lses]
    total = functools.reduce(jnp.add, weights)
    lse = top + jnp.log2(total)
    out = None
    for p, w, scale in zip(pieces, weights, scales):
        term = numbers(p[:, :rows, :]) * as_column(w / total * scale, rows // 2)
        out = term if out is None else out + term
    coded, exponent = encode(out)
    o_ref[:, :rows, :] = coded.astype(I16)
    chunks, per = out.shape[0], rows // 2
    spread = jnp.broadcast_to(exponent, (chunks, rows, 128)).reshape(chunks, 2, per, 128)
    exponents = jnp.sum(jnp.where(diagonal(per)[None, None], spread, 0.0), axis=2)
    write_stats(o_ref, [lse[:, kv] for kv in range(2)], [exponents[:, kv] for kv in range(2)])


def final_kernel(p_ref, o_ref):
    rows = o_ref.shape[0]
    lse, scale = read_stats(p_ref[:, rows:, :])
    top = jnp.max(lse, axis=0, keepdims=True)
    weights = jnp.exp2(lse - top)
    weights = weights / jnp.sum(weights, axis=0, keepdims=True)
    column = as_column(weights * scale, rows // 2)
    o_ref[...] = jnp.sum(numbers(p_ref[:, :rows, :]) * column, axis=0).astype(BF16)


def attend(lengths, q, keys, values, new_keys, new_values, bias):
    tokens, kv_heads, group, width = q.shape
    rows = tokens * group
    slots = keys.shape[2]
    chunk_rows = rows // NZ * kv_heads
    vmem = pl.BlockSpec(memory_space=pltpu.VMEM)
    return pl.pallas_call(
        attend_kernel,
        out_shape=jax.ShapeDtypeStruct((NZ, chunk_rows + STAT_ROWS, width), I16),
        in_specs=[pl.BlockSpec(memory_space=pltpu.SMEM)] + [vmem] * 6,
        out_specs=vmem,
        scratch_shapes=[
            pltpu.VMEM((rows, slots), F32),
            pltpu.VMEM((rows, 128), F32),
            pltpu.VMEM((2, rows, 2 * width), F32),
            pltpu.VMEM((2, rows, 128), F32),
            pltpu.VMEM((2, kv_heads, NZ, 128), F32),
        ],
        compiler_params=pltpu.CompilerParams(vmem_limit_bytes=32 * 1024 * 1024),
        cost_estimate=pl.CostEstimate(
            flops=4 * rows * kv_heads * slots * 2 * width,
            bytes_accessed=2 * (keys.size + values.size),
            transcendentals=rows * kv_heads * slots,
        ),
        name="attend",
    )(lengths, q, keys, values, new_keys, new_values, bias)


def merge(pieces):
    return pl.pallas_call(
        merge_kernel,
        out_shape=jax.ShapeDtypeStruct(pieces[0].shape, I16),
        in_specs=[pl.BlockSpec(memory_space=pltpu.VMEM)] * len(pieces),
        out_specs=pl.BlockSpec(memory_space=pltpu.VMEM),
        cost_estimate=pl.CostEstimate(flops=8 * pieces[0].size, bytes_accessed=10 * pieces[0].size, transcendentals=0),
        name="merge",
    )(*pieces)


def finish(pieces):
    return pl.pallas_call(
        final_kernel,
        out_shape=jax.ShapeDtypeStruct((pieces.shape[1] - STAT_ROWS, HEAD_WIDTH), BF16),
        in_specs=[pl.BlockSpec(memory_space=pltpu.VMEM)],
        out_specs=pl.BlockSpec(memory_space=pltpu.VMEM),
        cost_estimate=pl.CostEstimate(flops=4 * pieces.size, bytes_accessed=2 * pieces.size, transcendentals=0),
        name="finish",
    )(pieces)


def along_x(a, step):
    return lax.ppermute(a, "x", [(i, (i - step) % NX) for i in range(NX)])


def body(queries, fresh_keys, fresh_values, cache_keys, stored_values, cache_lengths, positions):
    x, z, core = lax.axis_index("x"), lax.axis_index("z"), lax.axis_index("core")
    width, group = HEAD_WIDTH, HEADS_PER_GROUP
    kv_mine = fresh_keys.shape[1] // width // 2
    slots = cache_keys.shape[0]

    def halves(a):
        half = a.shape[1] // 2
        first, second = a[:, :half], a[:, half:]
        return jnp.where(core == 0, first, second), jnp.where(core == 0, second, first)

    keep, give = halves(queries)
    got = lax.ppermute(give, "core", SWAP)
    mine = jnp.stack([keep, got]).reshape(2, kv_mine, group, width)

    k_keep, k_give = halves(cache_keys)
    v_keep, v_give = halves(stored_values)

    def by_head(a):
        return a.reshape(a.shape[0], kv_mine, width).transpose(1, 0, 2)

    kv_keep = jnp.stack([by_head(k_keep), by_head(v_keep)])
    kv_give = jnp.stack([by_head(k_give), by_head(v_give)])
    kv_got = lax.ppermute(kv_give, "core", SWAP)
    keys = jnp.stack([kv_keep[0], kv_got[0]])
    values = jnp.stack([kv_keep[1], kv_got[1]])
    new_keep, new_give = halves(jnp.concatenate([fresh_keys, fresh_values], axis=0))
    new_got = lax.ppermute(new_give, "core", SWAP)
    new = jnp.stack([new_keep, new_got])
    new = new.reshape(2, 2, kv_mine, width).transpose(1, 2, 0, 3)
    new = jnp.pad(new, ((0, 0), (0, 0), (0, 128 - 2), (0, 0)))
    lengths = jnp.concatenate([cache_lengths, lax.ppermute(cache_lengths, "core", SWAP)])

    table = positions.reshape(NX, NZ, 2)
    table = jnp.where(core == 0, table, table[:, :, ::-1])
    here = lax.dynamic_slice(table, (x, z, 0), (1, 1, 2)).reshape(2)
    lane = jnp.arange(128, dtype=jnp.int32)

    def bias_of(step):
        there = lax.dynamic_slice(table, (lax.rem(x + step, NX), 0, 0), (1, NZ, 2)).reshape(1, NZ * 2, 1)
        seen = (here[:, None, None] <= there) & (lane[None, None, :] == jnp.arange(2)[:, None, None])
        return jnp.where(seen, 0.0, -jnp.inf).astype(F32)

    column = lax.all_to_all(jnp.broadcast_to(mine[None], (NZ, *mine.shape)), "z", 0, 0, tiled=True)
    column = column.reshape(NZ * 2, kv_mine, group, width)
    steps = (0, 1, 3, 2)
    asked = [column if s == 0 else along_x(column, s) for s in steps]
    results = [attend(lengths, q, keys, values, new[0], new[1], bias_of(s)) for q, s in zip(asked, steps)]
    pieces = [r if s == 0 else along_x(r, -s) for r, s in zip(results, steps)]
    merged = merge(pieces)
    merged = lax.all_to_all(merged, "z", 0, 0, tiled=True)
    done = finish(merged).reshape(kv_mine, 2, group * width)
    own, other = done[:, 0].reshape(1, -1), done[:, 1].reshape(1, -1)
    back = lax.ppermute(other, "core", SWAP)
    return jnp.where(core == 0, jnp.concatenate([own, back], 1), jnp.concatenate([back, own], 1))


def solution(mesh):
    finer = Mesh(mesh.devices.reshape(mesh.shape["groups"], NX, NZ, 2), GROUPS_CTX)
    return jax.shard_map(
        body,
        mesh=finer,
        in_specs=(
            P(GROUPS_CTX, None),
            P(GROUPS_CTX, None),
            P(GROUPS_CTX, None),
            P(GROUPS_CTX, None),
            P(GROUPS_CTX, None),
            P(GROUPS_CTX),
            P("groups"),
        ),
        out_specs=P(GROUPS_CTX, None),
        check_vma=False,
    )
```

time: 460 us -> 124 us (0.27)
  blocking collectives: 222 us -> 25.4 us
  waiting for transfers between devices: 96.2 us -> 15.2 us
  local copies, waits for them, and re-layouts: 58.1 us -> 9.6 us
  starting transfers between devices: 0.07 us -> 44.6 us
  matrix products: 41.7 us -> 0 us
  Pallas kernels: 0 us -> 22.9 us
  other arithmetic: 25.1 us -> 4.19 us
  between operations: 14.4 us -> 0.99 us
    all_to_all x1, blocking collectives: 211 us -> 25.4 us  [body(): merged = lax.all_to_all(merged, 'z', 0, 0, tiled=True)]
    all_gather x2 -> x0, waiting for transfers between devices: 96.1 us -> none  [stacked_from(): tiles = lax.all_gather(tiles, axes[k])]
    dot_general x8 -> x0, matrix products: 41.7 us -> none  [the longest x4 27.5 us: body(): jnp.einsum('ngd,kd->ngk', query_part, key_part, preferred_element_type=jn...]
    ppermute x0 -> x11, starting transfers between devices: none -> 39.9 us  [the longest x1 20.4 us: body(): kv_got = lax.ppermute(kv_give, 'core', SWAP)]
    concatenate x4 -> x0, local copies, waits for them, and re-layouts: 27.3 us -> none  [the longest x1 25.9 us: side_by_side(): both = jnp.concatenate(arrays, axis=along)]
    pallas_call x0 -> x6, Pallas kernels: none -> 22.9 us  [the longest x4 18.2 us: attend(): pl.pallas_call(attend_kernel, out_shape=jax.ShapeDtypeStruct((NZ, chunk_r...]
    reduce_sum x3 -> x0, other arithmetic: 21.2 us -> none  [the longest x1 12.7 us: body(): totals = jnp.sum(weights.astype(jnp.float32), axis=-1)]
    all_to_all x0 -> x1, waiting for transfers between devices: none -> 12.9 us  [body(): lax.all_to_all(jnp.broadcast_to(mine[None], (NZ, *mine.shape)), 'z', 0, 0...]
  transfers between devices with their start and end apart: 2 -> 12, of which waited for: 2 -> 4; matrix products, arithmetic and copies ran while one was open for 1% -> 3% of each run, Pallas kernels for 0% -> 15%
where the time goes in v1:
time: 124 us; the launch traced here: 123 us
  starting transfers between devices  44.6 us (36%)
  blocking collectives  25.4 us (20%)
  Pallas kernels  22.9 us (18%)
  waiting for transfers between devices  15.2 us (12%)
  local copies, waits for them, and re-layouts  9.6 us (8%)
  other arithmetic  4.19 us (3%)
    all_to_all x1, blocking collectives, body(): merged = lax.all_to_all(merged, 'z', 0, 0, tiled=True)  25.4 us
    ppermute x1, starting transfers between devices, body(): kv_got = lax.ppermute(kv_give, 'core', SWAP)  20.4 us
    pallas_call x4, Pallas kernels, attend(): pl.pallas_call(attend_kernel, out_shape=jax.ShapeDtypeStruct((NZ, chunk_r...  18.2 us
    all_to_all x1, waiting for transfers between devices, body(): lax.all_to_all(jnp.broadcast_to(mine[None], (NZ, *mine.shape)), 'z', 0, 0...  12.9 us
    ppermute x6, starting transfers between devices, along_x(): return lax.ppermute(a, 'x', [(i, (i - step) % NX) for i in range(NX)])  11 us
    ppermute x1, starting transfers between devices, body(): back = lax.ppermute(other, 'core', SWAP)  7.62 us
    all_to_all x1, starting transfers between devices, body(): lax.all_to_all(jnp.broadcast_to(mine[None], (NZ, *mine.shape)), 'z', 0, 0...  4.71 us
    unnamed x24, local copies, waits for them, and re-layouts  3.88 us
  transfers between devices with their start and end apart: 12, of which 4 were waited for; matrix products, arithmetic and copies ran while one was open for 3% of the time, Pallas kernels for 15%

profile of v1, /device:TPU:33, one launch (start us, length us, event | category | flops | bytes accessed | tf_op | source)
XLA Modules:
  0.0 122.9 jit_solution(17909825031743175524)
XLA Ops:
  0.0 1.3 %fusion.7 = (bf16[1024,256]{1,0:T(8,128)(2,1)S(1)}, bf16[1024,256]{1,0:T(8,128)(2,1)S(1)}) fusion(bf16[1024,512]{1,0:T(8,128)(2,1)} %param.10), kind=kLoop, calls=%fused_computation.41 | loop fusion | bytes 2097152 | tf_op jit(solution)/shard_map/slice | solution.py:231
  1.7 0.8 copy-done.2
  3.0 1.2 broadcast_select_fusion
  4.2 1.4 %copy.14 = bf16[1024,2,128]{2,0,1:T(8,128)(2,1)S(1)} copy(bf16[1024,2,128]{0,2,1:T(8,128)(2,1)} %bitcast.38) | data formatting | bytes 1048576 | tf_op jit(solution)/shard_map/reshape | solution.py:242
  5.9 1.1 pad_maximum_fusion
  7.0 20.4 %collective-permute-start.2 = (bf16[2,2,1024,128]{3,2,1,0:T(8,128)(2,1)}, bf16[2,2,1024,128]{3,2,1,0:T(8,128)(2,1)S(1)}, u32[]{:S(2)}, u32[]{:S(2)}) collective-permute-start(bf16[2,2,1024,128]{3,2,1,0:T(8,128)(2,1)} %pad_maximum_fusion), channel_id=1, source_target_pairs={{0,1},{1,0},{2,3},{3,2},{4,5},{5,4},{6,7},{7,6},{8,9},{9,8},{10,11... | collective-permute-start | bytes 3145736 | tf_op jit(solution)/shard_map/ppermute | solution.py:246
  27.6 0.6 collective-permute-start.1
  28.4 0.7 copy-done.9
  31.0 0.8 broadcast_in_dim.30
  31.7 4.7 %all-to-all-start = ((bf16[16,2,2,16,128]{4,3,2,1,0:T(8,128)(2,1)}), bf16[16,2,2,16,128]{4,3,2,1,0:T(8,128)(2,1)S(1)}, u32[]{:S(2)}, u32[]{:S(2)}) async-start(bf16[16,2,2,16,128]{4,3,2,1,0:T(8,128)(2,1)} %broadcast_in_dim.30), calls=%async_computation | async-start | bytes 524288 | tf_op jit(solution)/shard_map/all_to_all | solution.py:266
  36.7 0.7 pad_add_fusion.len_ref
  37.4 12.9 %all-to-all-done = bf16[16,2,2,16,128]{4,3,2,1,0:T(8,128)(2,1)S(1)} async-done(((bf16[16,2,2,16,128]{4,3,2,1,0:T(8,128)(2,1)}), bf16[16,2,2,16,128]{4,3,2,1,0:T(8,128)(2,1)S(1)}, u32[]{:S(2)}, u32[]{:S(2)}) %all-to-all-start) | async-done | bytes 262176 | tf_op jit(solution)/shard_map/all_to_all | solution.py:266
  50.3 3.0 %collective-permute-start.8 = (bf16[32,2,16,128]{3,2,1,0:T(8,128)(2,1)S(1)}, bf16[32,2,16,128]{3,2,1,0:T(8,128)(2,1)S(1)}, u32[]{:S(2)}, u32[]{:S(2)}) collective-permute-start(bf16[32,2,16,128]{3,2,1,0:T(8,128)(2,1)S(1)} %bitcast.31), channel_id=1, source_target_pairs={{0,64},{32,96},{64,0},{96,32},{1,65},{33,97},{65,1},{97,33},{2,66}... | collective-permute-start | bytes 786440 | tf_op jit(solution)/shard_map/ppermute | solution.py:220
  53.7 2.2 %collective-permute-start.4 = (bf16[32,2,16,128]{3,2,1,0:T(8,128)(2,1)S(1)}, bf16[32,2,16,128]{3,2,1,0:T(8,128)(2,1)S(1)}, u32[]{:S(2)}, u32[]{:S(2)}) collective-permute-start(bf16[32,2,16,128]{3,2,1,0:T(8,128)(2,1)S(1)} %bitcast.33), channel_id=1, source_target_pairs={{0,96},{32,0},{64,32},{96,64},{1,97},{33,1},{65,33},{97,65},{2,98}... | collective-permute-start | bytes 786440 | tf_op jit(solution)/shard_map/ppermute | solution.py:220
  56.2 0.8 collective-permute-done.8.q_ref
  57.0 4.5 %attend.7 = s16[16,72,128]{2,1,0:T(8,128)(2,1)S(1)} custom-call(s32[2]{0:T(128)S(1)} %pad_add_fusion.len_ref, bf16[32,2,16,128]{3,2,1,0:T(8,128)(2,1)S(1)} %collective-permute-done.8.q_ref, bf16[2,2,1024,128]{3,2,1,0:T(8,128)(2,1)S(1)} %pad_maximum_fusion.1.k_ref, bf16[2,2,1024,128]{3,2,1,0:T(8,128)(2,1)S(1)} %pad_maximum_fusion.2.v_ref, ...), custom_call_target="tpu_custom_call" | custom-call | flops 1073741824 | bytes 2097152 | tf_op jit(solution)/shard_map/attend/pallas_call | solution.py:175
  61.6 3.3 %collective-permute-start.9 = (s16[16,72,128]{2,1,0:T(8,128)(2,1)S(1)}, s16[16,72,128]{2,1,0:T(8,128)(2,1)S(1)}, u32[]{:S(2)}, u32[]{:S(2)}) collective-permute-start(s16[16,72,128]{2,1,0:T(8,128)(2,1)S(1)} %attend.7), channel_id=1, source_target_pairs={{0,64},{32,96},{64,0},{96,32},{1,65},{33,97},{65,1},{97,33},{2,66}... | collective-permute-start | bytes 884744 | tf_op jit(solution)/shard_map/ppermute | solution.py:220
  64.9 4.5 %attend.6 = s16[16,72,128]{2,1,0:T(8,128)(2,1)S(1)} custom-call(s32[2]{0:T(128)S(1)} %pad_add_fusion.len_ref, bf16[32,2,16,128]{3,2,1,0:T(8,128)(2,1)S(1)} %collective-permute-done.6.q_ref, bf16[2,2,1024,128]{3,2,1,0:T(8,128)(2,1)S(1)} %pad_maximum_fusion.1.k_ref, bf16[2,2,1024,128]{3,2,1,0:T(8,128)(2,1)S(1)} %pad_maximum_fusion.2.v_ref, ...), custom_call_target="tpu_custom_call" | custom-call | flops 1073741824 | bytes 2097152 | tf_op jit(solution)/shard_map/attend/pallas_call | solution.py:175
  69.4 1.1 collective-permute-start.7
  70.6 4.5 %attend.5 = s16[16,72,128]{2,1,0:T(8,128)(2,1)S(1)} custom-call(s32[2]{0:T(128)S(1)} %pad_add_fusion.len_ref, bf16[32,2,16,128]{3,2,1,0:T(8,128)(2,1)S(1)} %collective-permute-done.4.q_ref, bf16[2,2,1024,128]{3,2,1,0:T(8,128)(2,1)S(1)} %pad_maximum_fusion.1.k_ref, bf16[2,2,1024,128]{3,2,1,0:T(8,128)(2,1)S(1)} %pad_maximum_fusion.2.v_ref, ...), custom_call_target="tpu_custom_call" | custom-call | flops 1073741824 | bytes 2097152 | tf_op jit(solution)/shard_map/attend/pallas_call | solution.py:175
  75.1 0.9 collective-permute-start.5
  76.0 4.5 %attend.4.refs_0_ = s16[16,72,128]{2,1,0:T(8,128)(2,1)S(1)} custom-call(s32[2]{0:T(128)S(1)} %pad_add_fusion.len_ref, bf16[32,2,16,128]{3,2,1,0:T(8,128)(2,1)S(1)} %bitcast.34, bf16[2,2,1024,128]{3,2,1,0:T(8,128)(2,1)S(1)} %pad_maximum_fusion.1.k_ref, bf16[2,2,1024,128]{3,2,1,0:T(8,128)(2,1)S(1)} %pad_maximum_fusion.2.v_ref, ...), custom_call_target="tpu_custom_call" | custom-call | flops 1073741824 | bytes 2097152 | tf_op jit(solution)/shard_map/attend/pallas_call | solution.py:175
  80.6 0.7 copy-done
  81.3 0.7 collective-permute-done.5.refs_1_
  82.2 0.7 copy-done.5
  82.9 2.9 %merge.1 = s16[16,72,128]{2,1,0:T(8,128)(2,1)} custom-call(s16[16,72,128]{2,1,0:T(8,128)(2,1)} %copy-done, s16[16,72,128]{2,1,0:T(8,128)(2,1)} %copy-done.5, s16[16,72,128]{2,1,0:T(8,128)(2,1)} %copy-done.4, s16[16,72,128]{2,1,0:T(8,128)(2,1)} %copy-done.3), custom_call_target="tpu_custom_call" | custom-call | flops 1179648 | bytes 1474560 | tf_op jit(solution)/shard_map/merge/pallas_call | solution.py:198
  85.8 25.4 %all_to_all.10.p_ref = s16[16,72,128]{2,1,0:T(8,128)(2,1)} all-to-all(s16[16,72,128]{2,1,0:T(8,128)(2,1)} %merge.1), channel_id=1, replica_groups=mesh['groups'=2,'x'=4,'z'=16,'core'=2] {'z'}, dimensions={0} | all-to-all | bytes 589824 | tf_op jit(solution)/shard_map/all_to_all | solution.py:273
  111.1 1.8 %finish.1 = bf16[64,128]{1,0:T(8,128)(2,1)} custom-call(s16[16,72,128]{2,1,0:T(8,128)(2,1)} %all_to_all.10.p_ref), custom_call_target="tpu_custom_call" | custom-call | flops 589824 | bytes 294912 | tf_op jit(solution)/shard_map/finish/pallas_call | solution.py:209
  113.0 0.7 reshape.257
  113.7 7.6 %collective-permute-start.10 = (bf16[1,4096]{1,0:T(2,128)(2,1)S(1)}, bf16[1,4096]{1,0:T(2,128)(2,1)S(1)}, u32[]{:S(2)}, u32[]{:S(2)}) collective-permute-start(bf16[1,4096]{1,0:T(2,128)(2,1)S(1)} %bitcast.46), channel_id=1, source_target_pairs={{0,1},{1,0},{2,3},{3,2},{4,5},{5,4},{6,7},{7,6},{8,9},{9,8},{10,11... | collective-permute-start | bytes 24584 | tf_op jit(solution)/shard_map/ppermute | solution.py:276
  121.3 0.8 collective-permute-done.10
  122.2 0.7 broadcast_select_fusion.4
  (60 shorter events, 3.9 us)
Async XLA Ops:
  1.3 1.2 copy-start.2
  4.2 1.4 %copy-start.1 = (bf16[1024,256]{0,1:T(8,128)(2,1)S(1)}, bf16[1024,256]{0,1:T(8,128)(2,1)}, u32[]{:S(2)}) copy-start(bf16[1024,256]{0,1:T(8,128)(2,1)} %get-tuple-element.36) | copy-start | bytes 1572868
  5.8 21.6 %copy-start.7 = (bf16[1,512]{1,0:T(2,128)(2,1)S(1)}, bf16[1,512]{1,0:T(2,128)(2,1)}, u32[]{:S(2)}) copy-start(bf16[1,512]{1,0:T(2,128)(2,1)} %param.9) | copy-start | bytes 3076
  5.8 21.5 %copy-start.8 = (bf16[1,512]{1,0:T(2,128)(2,1)S(1)}, bf16[1,512]{1,0:T(2,128)(2,1)}, u32[]{:S(2)}) copy-start(bf16[1,512]{1,0:T(2,128)(2,1)} %param.8) | copy-start | bytes 3076
  5.8 21.7 %copy-start.6 = (bf16[1,8192]{1,0:T(2,128)(2,1)S(1)}, bf16[1,8192]{1,0:T(2,128)(2,1)}, u32[]{:S(2)}) copy-start(bf16[1,8192]{1,0:T(2,128)(2,1)} %param.7) | copy-start | bytes 49156
  7.0 49.0 %collective-permute-start.2 = (bf16[2,2,1024,128]{3,2,1,0:T(8,128)(2,1)}, bf16[2,2,1024,128]{3,2,1,0:T(8,128)(2,1)S(1)}, u32[]{:S(2)}, u32[]{:S(2)}) collective-permute-start(bf16[2,2,1024,128]{3,2,1,0:T(8,128)(2,1)} %pad_maximum_fusion), channel_id=1, source_target_pairs={{0,1},{1,0},{2,3},{3,2},{4,5},{5,4},{6,7},{7,6},{8,9},{9,8},{10,11... | collective-permute-start | bytes 3145736 | tf_op jit(solution)/shard_map/ppermute | solution.py:246
  27.4 9.9 %collective-permute-start.3 = (bf16[2,256]{1,0:T(2,128)(2,1)S(1)}, bf16[2,256]{1,0:T(2,128)(2,1)S(1)}, u32[]{:S(2)}, u32[]{:S(2)}) collective-permute-start(bf16[2,256]{1,0:T(2,128)(2,1)S(1)} %broadcast_select_fusion.8), channel_id=1, source_target_pairs={{0,1},{1,0},{2,3},{3,2},{4,5},{5,4},{6,7},{7,6},{8,9},{9,8},{10,11... | collective-permute-start | bytes 3080 | tf_op jit(solution)/shard_map/ppermute | solution.py:250
  27.6 3.3 %collective-permute-start.1 = (bf16[1,4096]{1,0:T(2,128)(2,1)S(1)}, bf16[1,4096]{1,0:T(2,128)(2,1)S(1)}, u32[]{:S(2)}, u32[]{:S(2)}) collective-permute-start(bf16[1,4096]{1,0:T(2,128)(2,1)S(1)} %get-tuple-element.23), channel_id=1, source_target_pairs={{0,1},{1,0},{2,3},{3,2},{4,5},{5,4},{6,7},{7,6},{8,9},{9,8},{10,11... | collective-permute-start | bytes 24584 | tf_op jit(solution)/shard_map/ppermute | solution.py:235
  28.2 8.4 %collective-permute-start = (s32[1]{0:T(128)}, s32[1]{0:T(128)}, u32[]{:S(2)}, u32[]{:S(2)}) collective-permute-start(s32[1]{0:T(128)} %param.12), channel_id=1, source_target_pairs={{0,1},{1,0},{2,3},{3,2},{4,5},{5,4},{6,7},{7,6},{8,9},{9,8},{10,11... | collective-permute-start | bytes 20 | tf_op jit(solution)/shard_map/ppermute | solution.py:254
  28.4 0.7 copy-start.9
  31.7 18.5 %all-to-all-start = ((bf16[16,2,2,16,128]{4,3,2,1,0:T(8,128)(2,1)}), bf16[16,2,2,16,128]{4,3,2,1,0:T(8,128)(2,1)S(1)}, u32[]{:S(2)}, u32[]{:S(2)}) async-start(bf16[16,2,2,16,128]{4,3,2,1,0:T(8,128)(2,1)} %broadcast_in_dim.30), calls=%async_computation | async-start | bytes 524288 | tf_op jit(solution)/shard_map/all_to_all | solution.py:266
  50.3 6.8 %collective-permute-start.8 = (bf16[32,2,16,128]{3,2,1,0:T(8,128)(2,1)S(1)}, bf16[32,2,16,128]{3,2,1,0:T(8,128)(2,1)S(1)}, u32[]{:S(2)}, u32[]{:S(2)}) collective-permute-start(bf16[32,2,16,128]{3,2,1,0:T(8,128)(2,1)S(1)} %bitcast.31), channel_id=1, source_target_pairs={{0,64},{32,96},{64,0},{96,32},{1,65},{33,97},{65,1},{97,33},{2,66}... | collective-permute-start | bytes 786440 | tf_op jit(solution)/shard_map/ppermute | solution.py:220
  53.3 11.6 %collective-permute-start.6 = (bf16[32,2,16,128]{3,2,1,0:T(8,128)(2,1)S(1)}, bf16[32,2,16,128]{3,2,1,0:T(8,128)(2,1)S(1)}, u32[]{:S(2)}, u32[]{:S(2)}) collective-permute-start(bf16[32,2,16,128]{3,2,1,0:T(8,128)(2,1)S(1)} %bitcast.32), channel_id=1, source_target_pairs={{0,32},{32,64},{64,96},{96,0},{1,33},{33,65},{65,97},{97,1},{2,34}... | collective-permute-start | bytes 786440 | tf_op jit(solution)/shard_map/ppermute | solution.py:220
  53.7 16.8 %collective-permute-start.4 = (bf16[32,2,16,128]{3,2,1,0:T(8,128)(2,1)S(1)}, bf16[32,2,16,128]{3,2,1,0:T(8,128)(2,1)S(1)}, u32[]{:S(2)}, u32[]{:S(2)}) collective-permute-start(bf16[32,2,16,128]{3,2,1,0:T(8,128)(2,1)S(1)} %bitcast.33), channel_id=1, source_target_pairs={{0,96},{32,0},{64,32},{96,64},{1,97},{33,1},{65,33},{97,65},{2,98}... | collective-permute-start | bytes 786440 | tf_op jit(solution)/shard_map/ppermute | solution.py:220
  61.6 19.7 %collective-permute-start.9 = (s16[16,72,128]{2,1,0:T(8,128)(2,1)S(1)}, s16[16,72,128]{2,1,0:T(8,128)(2,1)S(1)}, u32[]{:S(2)}, u32[]{:S(2)}) collective-permute-start(s16[16,72,128]{2,1,0:T(8,128)(2,1)S(1)} %attend.7), channel_id=1, source_target_pairs={{0,64},{32,96},{64,0},{96,32},{1,65},{33,97},{65,1},{97,33},{2,66}... | collective-permute-start | bytes 884744 | tf_op jit(solution)/shard_map/ppermute | solution.py:220
  69.4 11.9 %collective-permute-start.7 = (s16[16,72,128]{2,1,0:T(8,128)(2,1)S(1)}, s16[16,72,128]{2,1,0:T(8,128)(2,1)S(1)}, u32[]{:S(2)}, u32[]{:S(2)}) collective-permute-start(s16[16,72,128]{2,1,0:T(8,128)(2,1)S(1)} %attend.6), channel_id=1, source_target_pairs={{0,96},{32,0},{64,32},{96,64},{1,97},{33,1},{65,33},{97,65},{2,98}... | collective-permute-start | bytes 884744 | tf_op jit(solution)/shard_map/ppermute | solution.py:220
  75.1 6.9 %collective-permute-start.5 = (s16[16,72,128]{2,1,0:T(8,128)(2,1)S(1)}, s16[16,72,128]{2,1,0:T(8,128)(2,1)S(1)}, u32[]{:S(2)}, u32[]{:S(2)}) collective-permute-start(s16[16,72,128]{2,1,0:T(8,128)(2,1)S(1)} %attend.5), channel_id=1, source_target_pairs={{0,32},{32,64},{64,96},{96,0},{1,33},{33,65},{65,97},{97,1},{2,34}... | collective-permute-start | bytes 884744 | tf_op jit(solution)/shard_map/ppermute | solution.py:220
  80.6 0.7 copy-start
  81.3 0.7 copy-start.3
  81.3 0.8 copy-start.4
  82.2 0.7 copy-start.5
  113.7 8.5 %collective-permute-start.10 = (bf16[1,4096]{1,0:T(2,128)(2,1)S(1)}, bf16[1,4096]{1,0:T(2,128)(2,1)S(1)}, u32[]{:S(2)}, u32[]{:S(2)}) collective-permute-start(bf16[1,4096]{1,0:T(2,128)(2,1)S(1)} %bitcast.46), channel_id=1, source_target_pairs={{0,1},{1,0},{2,3},{3,2},{4,5},{5,4},{6,7},{7,6},{8,9},{9,8},{10,11... | collective-permute-start | bytes 24584 | tf_op jit(solution)/shard_map/ppermute | solution.py:276

commit v2 on v1

v2 whole, which is shorter than its diff:
```python
import functools
import math

import jax
import jax.numpy as jnp
from jax import lax
from jax.experimental import pallas as pl
from jax.experimental.pallas import tpu as pltpu
from jax.sharding import Mesh
from jax.sharding import PartitionSpec as P

HEADS_PER_GROUP = 16
HEAD_WIDTH = 128
GROUPS_CTX = ("groups", "x", "z", "core")
NX, NZ = 4, 16
LOG2_SCALE = HEAD_WIDTH ** (-0.5) * math.log2(math.e)
STAT_ROWS = 8
LSE_STEPS = 2.0**18
FULL = 32767.0
F32, BF16, I16, I32 = jnp.float32, jnp.bfloat16, jnp.int16, jnp.int32
SWAP = [(0, 1), (1, 0)]
CHUNK = 256
HIDDEN = -(2.0**100)


def dot_nt(a, b):
    return lax.dot_general(a, b, (((1,), (1,)), ((), ())), preferred_element_type=F32)


def dot_nn(a, b):
    return lax.dot_general(a, b, (((1,), (0,)), ((), ())), preferred_element_type=F32)


def diagonal(rows):
    row = lax.broadcasted_iota(jnp.int32, (rows, 128), 0)
    lane = lax.broadcasted_iota(jnp.int32, (rows, 128), 1)
    return lax.rem(lane, rows) == row


def attend_kernel(n_ref, q_ref, qm_ref, k_ref, km_ref, v_ref, o_ref, qa_scr, s_scr, m_scr, acc_scr, st_scr):
    tokens, kv_heads, group, width = q_ref.shape
    rows = tokens * group
    tile = rows // 2
    chunks = o_ref.shape[0]
    per = rows // chunks
    units = [(kv, slice(r, r + tile)) for kv in range(kv_heads) for r in range(0, rows, tile)]

    for kv in range(kv_heads):
        qa_scr[kv, :, :width] = q_ref[:, kv].reshape(rows, width)
        mask = jnp.broadcast_to(qm_ref[...][:, None, :], (tokens, group, 128))
        qa_scr[kv, :, width:] = mask.reshape(rows, 128).astype(BF16)

    @pl.loop(0, 2)
    def block(blk):
        def variant(slots):
            spans = [slice(c, min(c + CHUNK, slots)) for c in range(0, slots, CHUNK)]
            tops = []
            for kv, r in units:
                top = None
                for span in spans:
                    head = slice(kv * width, (kv + 1) * width)
                    k = jnp.concatenate([k_ref[blk, span, head], km_ref[blk, span, :]], axis=1)
                    s = dot_nt(qa_scr[kv, r], k)
                    s_scr[kv, r, span] = s
                    for l in range(0, s.shape[1], 128):
                        part = s[:, l : l + 128]
                        top = part if top is None else jnp.maximum(top, part)
                m_scr[blk, kv, r] = top
            for kv, r in units:
                top = jnp.max(m_scr[blk, kv, r], axis=1, keepdims=True)
                acc = None
                for span in spans:
                    p = jnp.exp2((s_scr[kv, r, span] - top) * LOG2_SCALE).astype(BF16)
                    v = v_ref[blk, span, kv * width : (kv + 1) * width]
                    term = dot_nn(p, jnp.concatenate([v, jnp.ones_like(v)], axis=1))
                    acc = term if acc is None else acc + term
                acc_scr[blk, kv, r] = acc
                m_scr[blk, kv, r] = jnp.broadcast_to(top * LOG2_SCALE, (tile, 128))

        used, low = n_ref[blk], 0
        full = k_ref.shape[1]
        for slots in (CHUNK, 2 * CHUNK, 3 * CHUNK, full):
            pl.when(jnp.logical_and(used > low, used <= slots))(functools.partial(variant, slots))
            low = slots

    @pl.loop(0, kv_heads)
    def close(kv):
        m_a, m_b = m_scr[0, kv], m_scr[1, kv]
        top = jnp.maximum(m_a, m_b)
        w_a, w_b = jnp.exp2(m_a - top), jnp.exp2(m_b - top)
        total = acc_scr[0, kv, :, width:] * w_a + acc_scr[1, kv, :, width:] * w_b
        mean = (acc_scr[0, kv, :, :width] * w_a + acc_scr[1, kv, :, :width] * w_b) / total
        lse = top + jnp.log2(total)
        at = pl.multiple_of(kv * per, per)
        coded, exponent = encode(mean)
        o_ref[:, pl.ds(at, per), :] = coded.reshape(chunks, per, width).astype(I16)
        pick = diagonal(per)[None]
        st_scr[0, kv] = jnp.sum(jnp.where(pick, lse.reshape(chunks, per, 128), 0.0), axis=1)
        spread = jnp.broadcast_to(exponent, (rows, 128)).reshape(chunks, per, 128)
        st_scr[1, kv] = jnp.sum(jnp.where(pick, spread, 0.0), axis=1)

    o_ref[:, kv_heads * per :, :] = stat_rows(
        [st_scr[0, kv] for kv in range(kv_heads)], [st_scr[1, kv] for kv in range(kv_heads)]
    )


def encode(mean):
    largest = jnp.max(jnp.abs(mean), axis=-1, keepdims=True)
    exponent = jnp.ceil(jnp.log2(jnp.maximum(largest, 1e-30)))
    return jnp.round(mean * (FULL * jnp.exp2(-exponent))).astype(I32), exponent


def stat_rows(lses, exponents):
    steps = [jnp.round(l * LSE_STEPS).astype(I32) for l in lses]
    terms = [lax.shift_right_arithmetic(t, jnp.full_like(t, 16)) for t in steps]
    terms += [(t & 0xFFFF) - 32768 for t in steps]
    terms += [e.astype(I32) for e in exponents]
    terms += [jnp.zeros_like(terms[0])] * (STAT_ROWS - len(terms))
    return jnp.stack(terms, axis=1).astype(I16)


def read_stats(stats):
    stats = stats.astype(I32)
    steps = stats[:, 0:2] * 65536 + (stats[:, 2:4] + 32768)
    return steps.astype(F32) * (1.0 / LSE_STEPS), jnp.exp2(stats[:, 4:6].astype(F32)) * (1.0 / FULL)


def as_column(w, per):
    chunks = w.shape[0]
    spread = jnp.broadcast_to(w[:, :, None, :], (chunks, 2, per, 128))
    lane = lax.broadcasted_iota(jnp.int32, (per, 128), 1)
    row = lax.broadcasted_iota(jnp.int32, (per, 128), 0)
    column = jnp.sum(jnp.where((lane == row)[None, None], spread, 0.0), axis=3, keepdims=True)
    return column.reshape(chunks, 2 * per, 1)


def numbers(coded):
    return coded.astype(I32).astype(F32)


def merge_kernel(*refs):
    pieces, o_ref = refs[:-1], refs[-1]
    rows = o_ref.shape[1] - STAT_ROWS
    per, at_once = rows // 2, 16

    for g in range(o_ref.shape[0] // at_once):
        here = slice(g * at_once, (g + 1) * at_once)
        lses, scales = zip(*[read_stats(p[here, rows:, :]) for p in pieces])
        top = functools.reduce(jnp.maximum, lses)
        weights = [jnp.exp2(l - top) for l in lses]
        total = functools.reduce(jnp.add, weights)
        lse = top + jnp.log2(total)
        out = None
        for p, w, scale in zip(pieces, weights, scales):
            term = numbers(p[here, :rows, :]) * as_column(w / total * scale, per)
            out = term if out is None else out + term
        coded, exponent = encode(out)
        o_ref[here, :rows, :] = coded.astype(I16)
        spread = jnp.broadcast_to(exponent, (at_once, rows, 128)).reshape(at_once, 2, per, 128)
        exponents = jnp.sum(jnp.where(diagonal(per)[None, None], spread, 0.0), axis=2)
        o_ref[here, rows:, :] = stat_rows([lse[:, kv] for kv in range(2)], [exponents[:, kv] for kv in range(2)])


def final_kernel(p_ref, o_ref):
    sources, rows, width = p_ref.shape
    rows -= STAT_ROWS
    lse, scale = read_stats(p_ref[:, rows:, :])
    lse = lse.reshape(sources // 2, 2, *lse.shape[1:])
    top = jnp.max(lse, axis=0, keepdims=True)
    weights = jnp.exp2(lse - top)
    weights = weights / jnp.sum(weights, axis=0, keepdims=True)
    column = as_column(weights.reshape(scale.shape) * scale, rows // 2)
    terms = (numbers(p_ref[:, :rows, :]) * column).reshape(sources // 2, 2 * rows, width)
    o_ref[...] = jnp.sum(terms, axis=0).astype(BF16)


VMEM_SPEC = pl.BlockSpec(memory_space=pltpu.VMEM)


def attend(counts, q, q_mask, keys, key_mask, values):
    tokens, kv_heads, group, width = q.shape
    rows = tokens * group
    slots = keys.shape[1]
    chunk_rows = kv_heads * group
    return pl.pallas_call(
        attend_kernel,
        out_shape=jax.ShapeDtypeStruct((tokens, chunk_rows + STAT_ROWS, width), I16),
        in_specs=[pl.BlockSpec(memory_space=pltpu.SMEM)] + [VMEM_SPEC] * 5,
        out_specs=VMEM_SPEC,
        scratch_shapes=[
            pltpu.VMEM((kv_heads, rows, width + 128), BF16),
            pltpu.VMEM((kv_heads, rows, slots), F32),
            pltpu.VMEM((2, kv_heads, rows, 128), F32),
            pltpu.VMEM((2, kv_heads, rows, 2 * width), F32),
            pltpu.VMEM((2, kv_heads, tokens, 128), F32),
        ],
        compiler_params=pltpu.CompilerParams(vmem_limit_bytes=32 * 1024 * 1024),
        cost_estimate=pl.CostEstimate(
            flops=4 * rows * kv_heads * slots * 2 * width,
            bytes_accessed=2 * (keys.size + values.size),
            transcendentals=rows * kv_heads * slots,
        ),
        name="attend",
    )(counts, q, q_mask, keys, key_mask, values)


def merge(pieces):
    return pl.pallas_call(
        merge_kernel,
        out_shape=jax.ShapeDtypeStruct(pieces[0].shape, I16),
        in_specs=[VMEM_SPEC] * len(pieces),
        out_specs=VMEM_SPEC,
        compiler_params=pltpu.CompilerParams(vmem_limit_bytes=8 * 1024 * 1024),
        cost_estimate=pl.CostEstimate(flops=8 * pieces[0].size, bytes_accessed=10 * pieces[0].size, transcendentals=0),
        name="merge",
    )(*pieces)


def finish(pieces):
    return pl.pallas_call(
        final_kernel,
        out_shape=jax.ShapeDtypeStruct((2 * (pieces.shape[1] - STAT_ROWS), HEAD_WIDTH), BF16),
        in_specs=[VMEM_SPEC],
        out_specs=VMEM_SPEC,
        compiler_params=pltpu.CompilerParams(vmem_limit_bytes=4 * 1024 * 1024),
        cost_estimate=pl.CostEstimate(flops=4 * pieces.size, bytes_accessed=2 * pieces.size, transcendentals=0),
        name="finish",
    )(pieces)


def along_x(a, step):
    return lax.ppermute(a, "x", [(i, (i - step) % NX) for i in range(NX)])


def body(queries, fresh_keys, fresh_values, cache_keys, stored_values, cache_lengths, positions):
    x, z, core = lax.axis_index("x"), lax.axis_index("z"), lax.axis_index("core")
    width, group = HEAD_WIDTH, HEADS_PER_GROUP
    kv_mine = fresh_keys.shape[1] // width // 2
    slots = cache_keys.shape[0]
    padded = slots + 128

    def half(a, which):
        size = a.shape[1] // 2
        return lax.dynamic_slice_in_dim(a, which * size, size, 1)

    with jax.named_scope("ask"):
        split = queries.reshape(1, 2, kv_mine, group, width)
        split = jnp.broadcast_to(split, (NZ, *split.shape[1:])).reshape(NZ * 2, kv_mine, group, width)
        column = lax.all_to_all(split, ("z", "core"), 0, 0, tiled=True)

    with jax.named_scope("swapped"):
        given = jnp.stack([half(cache_keys, 1 - core), half(stored_values, 1 - core)])
        kv_got = lax.ppermute(given, "core", SWAP)
    with jax.named_scope("newer"):
        fresh = jnp.concatenate([fresh_keys, fresh_values], axis=0)
        new = jnp.stack([half(fresh, core), lax.ppermute(half(fresh, 1 - core), "core", SWAP)])
    with jax.named_scope("lengths"):
        lengths = jnp.concatenate([cache_lengths, lax.ppermute(cache_lengths, "core", SWAP)])
    slot = jnp.arange(padded, dtype=I32)

    def extended(own, other, added):
        both = jnp.pad(jnp.stack([own, other]), ((0, 0), (0, padded - slots), (0, 0)))
        return jnp.where((slot[None, :] == lengths[:, None])[:, :, None], added[:, None, :], both)

    keys = extended(half(cache_keys, core), kv_got[0], new[:, 0])
    values = extended(half(stored_values, core), kv_got[1], new[:, 1])

    table = positions.reshape(NX, NZ * 2)
    here = lax.dynamic_slice(table, (x, z * 2), (1, 2)).reshape(2)
    here = jnp.where(core == 0, here, here[::-1])
    lane = jnp.arange(128, dtype=I32)
    new_lane = jnp.where(here > 0, here, -1)
    hide = jnp.where(slot[None, :] < lengths[:, None], -1, jnp.where(slot[None, :] == lengths[:, None], new_lane[:, None], 0))
    key_mask = jnp.where(lane[None, None, :] == hide[:, :, None], HIDDEN, 0.0).astype(BF16)
    counts = lengths + 1

    def q_mask(step):
        there = lax.dynamic_slice(table, (lax.rem(x + step, NX), 0), (1, NZ * 2)).reshape(NZ * 2, 1)
        return jnp.where((lane[None, :] > there) | (lane[None, :] == 0), 1.0, 0.0).astype(F32)

    steps = (0, 1, 3, 2)
    asked = [column if s == 0 else along_x(column, s) for s in steps]
    results = [attend(counts, q, q_mask(s), keys, key_mask, values) for q, s in zip(asked, steps)]
    pieces = [r if s == 0 else along_x(r, -s) for r, s in zip(results, steps)]
    merged = lax.all_to_all(merge(pieces), ("z", "core"), 0, 0, tiled=True)
    return finish(merged).reshape(1, -1)


def solution(mesh):
    finer = Mesh(mesh.devices.reshape(mesh.shape["groups"], NX, NZ, 2), GROUPS_CTX)
    return jax.shard_map(
        body,
        mesh=finer,
        in_specs=(
            P(GROUPS_CTX, None),
            P(GROUPS_CTX, None),
            P(GROUPS_CTX, None),
            P(GROUPS_CTX, None),
            P(GROUPS_CTX, None),
            P(GROUPS_CTX),
            P("groups"),
        ),
        out_specs=P(GROUPS_CTX, None),
        check_vma=False,
    )
```

time: 124 us -> 117 us (0.944)
  waiting for transfers between devices: 15.2 us -> 25.6 us
  Pallas kernels: 22.9 us -> 12.8 us
  starting transfers between devices: 44.6 us -> 37.7 us
  blocking collectives: 25.4 us -> 32 us
  local copies, waits for them, and re-layouts: 9.6 us -> 3.42 us
    pallas_call x5, Pallas kernels: 20 us -> 11.7 us  [the longest x4 11.4 us: attend(): pl.pallas_call(attend_kernel, out_shape=jax.ShapeDtypeStruct((tokens, chu...]
    ppermute x4 -> x2, starting transfers between devices: 28.8 us -> 20.5 us  [the longest x1 20.5 us: body(): lax.ppermute(half(fresh, 1 - core), 'core', SWAP)]
    all_to_all x1, waiting for transfers between devices: 12.9 us -> 19.6 us  [body(): column = lax.all_to_all(split, ('z', 'core'), 0, 0, tiled=True)]
    all_to_all x1, blocking collectives: 25.4 us -> 32 us  [body(): merged = lax.all_to_all(merge(pieces), ('z', 'core'), 0, 0, tiled=True)]
    ppermute x6, waiting for transfers between devices: 1.48 us -> 5.97 us  [along_x(): return lax.ppermute(a, 'x', [(i, (i - step) % NX) for i in range(NX)])]
    unnamed x24 -> x6, local copies, waits for them, and re-layouts: 3.88 us -> 0.66 us
    reshape x6 -> x2, local copies, waits for them, and re-layouts: 3.03 us -> 0.16 us  [the longest x1 0.08 us: body(): table = positions.reshape(NX, NZ * 2)]
    pallas_call x1, Pallas kernels: 2.87 us -> 1.13 us  [merge(): pl.pallas_call(merge_kernel, out_shape=jax.ShapeDtypeStruct(pieces[0].sha...]
  transfers between devices with their start and end apart: 12 -> 10, of which waited for: 4 -> 4; matrix products, arithmetic and copies ran while one was open for 3% -> 5% of each run, Pallas kernels for 15% -> 10%
where the time goes in v2:
time: 117 us
  starting transfers between devices  37.7 us (32%)
  blocking collectives  32 us (27%)
  waiting for transfers between devices  25.6 us (22%)
  Pallas kernels  12.8 us (11%)
  other arithmetic  4.38 us (4%)
  local copies, waits for them, and re-layouts  3.42 us (3%)
    all_to_all x1, blocking collectives, body(): merged = lax.all_to_all(merge(pieces), ('z', 'core'), 0, 0, tiled=True)  32 us
    ppermute x1, starting transfers between devices, body(): lax.ppermute(half(fresh, 1 - core), 'core', SWAP)  20.5 us
    all_to_all x1, waiting for transfers between devices, body(): column = lax.all_to_all(split, ('z', 'core'), 0, 0, tiled=True)  19.6 us
    ppermute x6, starting transfers between devices, along_x(): return lax.ppermute(a, 'x', [(i, (i - step) % NX) for i in range(NX)])  11.5 us
    pallas_call x4, Pallas kernels, attend(): pl.pallas_call(attend_kernel, out_shape=jax.ShapeDtypeStruct((tokens, chu...  11.4 us
    ppermute x6, waiting for transfers between devices, along_x(): return lax.ppermute(a, 'x', [(i, (i - step) % NX) for i in range(NX)])  5.97 us
    all_to_all x1, starting transfers between devices, body(): column = lax.all_to_all(split, ('z', 'core'), 0, 0, tiled=True)  5.17 us
  transfers between devices with their start and end apart: 10, of which 4 were waited for; matrix products, arithmetic and copies ran while one was open for 5% of the time, Pallas kernels for 10%

profile of v2, /device:TPU:33, one launch (start us, length us, event | category | flops | bytes accessed | tf_op | source)
XLA Modules:
  0.0 116.8 jit_solution(9497194816897888817)
XLA Ops:
  0.0 0.8 fusion.18
  0.8 20.5 %collective-permute-start.1 = (bf16[2,256]{1,0:T(2,128)(2,1)S(1)}, bf16[2,256]{1,0:T(2,128)(2,1)S(1)}, u32[]{:S(2)}, u32[]{:S(2)}) collective-permute-start(bf16[2,256]{1,0:T(2,128)(2,1)S(1)} %get-tuple-element.16), channel_id=1, source_target_pairs={{0,1},{1,0},{2,3},{3,2},{4,5},{5,4},{6,7},{7,6},{8,9},{9,8},{10,11... | collective-permute-start | bytes 3080 | tf_op jit(solution)/shard_map/newer/ppermute | solution.py:256
  21.3 1.7 %dynamic-slice_bitcast_fusion = (bf16[1,1024,256]{2,1,0:T(8,128)(2,1)S(1)}, bf16[1,1024,256]{2,1,0:T(8,128)(2,1)S(1)}, bf16[1,1024,256]{2,1,0:T(8,128)(2,1)S(1)}, bf16[1,1024,256]{2,1,0:T(8,128)(2,1)S(1)}) fusion(bf16[1024,512]{1,0:T(8,128)(2,1)} %param.11, s32[]{:T(128)S(6)} %select_n.82, s32[]{:T(128)S(6)} %select_n.83, bf16[1024,512]{1,0:T(8,128)(2,1)} %param.10), kind=kLoop, calls=%fused_computation.12 | loop fusion | bytes 4194312 | tf_op jit(solution)/shard_map/stack | solution.py:262
  23.0 1.1 pad_maximum_fusion
  24.1 0.5 collective-permute-start
  24.5 0.1 reduce
  24.6 0.8 broadcast_in_dim.99
  25.4 5.2 %all-to-all-start = ((bf16[32,2,16,128]{3,2,1,0:T(8,128)(2,1)}), bf16[32,2,16,128]{3,2,1,0:T(8,128)(2,1)S(1)}, u32[]{:S(2)}, u32[]{:S(2)}) async-start(bf16[32,2,16,128]{3,2,1,0:T(8,128)(2,1)} %bitcast), calls=%async_computation | async-start | bytes 524288 | tf_op jit(solution)/shard_map/ask/all_to_all | solution.py:249
  31.3 0.1 reshape.102
  31.4 0.1 rev.3
  31.6 0.1 fusion.15
  31.7 0.6 broadcast_add_fusion
  32.4 0.5 select_convert_fusion.km_ref
  33.1 19.6 %all-to-all-done.q_ref = bf16[32,2,16,128]{3,2,1,0:T(8,128)(2,1)S(1)} async-done(((bf16[32,2,16,128]{3,2,1,0:T(8,128)(2,1)}), bf16[32,2,16,128]{3,2,1,0:T(8,128)(2,1)S(1)}, u32[]{:S(2)}, u32[]{:S(2)}) %all-to-all-start) | async-done | bytes 262176 | tf_op jit(solution)/shard_map/ask/all_to_all | solution.py:249
  52.7 3.0 %collective-permute-start.7 = (bf16[32,2,16,128]{3,2,1,0:T(8,128)(2,1)S(1)}, bf16[32,2,16,128]{3,2,1,0:T(8,128)(2,1)S(1)}, u32[]{:S(2)}, u32[]{:S(2)}) collective-permute-start(bf16[32,2,16,128]{3,2,1,0:T(8,128)(2,1)S(1)} %all-to-all-done.q_ref), channel_id=1, source_target_pairs={{0,64},{32,96},{64,0},{96,32},{1,65},{33,97},{65,1},{97,33},{2,66}... | collective-permute-start | bytes 786440 | tf_op jit(solution)/shard_map/ppermute | solution.py:232
  55.7 0.4 collective-permute-start.5
  56.2 2.2 %collective-permute-start.3 = (bf16[32,2,16,128]{3,2,1,0:T(8,128)(2,1)S(1)}, bf16[32,2,16,128]{3,2,1,0:T(8,128)(2,1)S(1)}, u32[]{:S(2)}, u32[]{:S(2)}) collective-permute-start(bf16[32,2,16,128]{3,2,1,0:T(8,128)(2,1)S(1)} %all-to-all-done.q_ref), channel_id=1, source_target_pairs={{0,96},{32,0},{64,32},{96,64},{1,97},{33,1},{65,33},{97,65},{2,98}... | collective-permute-start | bytes 786440 | tf_op jit(solution)/shard_map/ppermute | solution.py:232
  58.5 1.0 fusion.7
  59.4 2.2 %collective-permute-done.7.q_ref = bf16[32,2,16,128]{3,2,1,0:T(8,128)(2,1)S(1)} collective-permute-done((bf16[32,2,16,128]{3,2,1,0:T(8,128)(2,1)S(1)}, bf16[32,2,16,128]{3,2,1,0:T(8,128)(2,1)S(1)}, u32[]{:S(2)}, u32[]{:S(2)}) %collective-permute-start.7) | collective-permute-done | bytes 262176 | tf_op jit(solution)/shard_map/ppermute | solution.py:232
  61.6 2.8 %attend.7 = s16[32,40,128]{2,1,0:T(8,128)(2,1)S(1)} custom-call(s32[2]{0:T(128)S(1)} %get-tuple-element.5.n_ref, bf16[32,2,16,128]{3,2,1,0:T(8,128)(2,1)S(1)} %collective-permute-done.7.q_ref, f32[32,128]{1,0:T(8,128)S(1)} %get-tuple-element.23.qm_ref, bf16[2,1152,256]{2,1,0:T(8,128)(2,1)S(1)} %get-tuple-element.14.k_ref, ...), custom_call_target="tpu_custom_call" | custom-call | flops 1207959552 | bytes 2359296 | tf_op jit(solution)/shard_map/attend/pallas_call | solution.py:185
  64.5 3.9 %collective-permute-start.8 = (s16[32,40,128]{2,1,0:T(8,128)(2,1)S(1)}, s16[32,40,128]{2,1,0:T(8,128)(2,1)S(1)}, u32[]{:S(2)}, u32[]{:S(2)}) collective-permute-start(s16[32,40,128]{2,1,0:T(8,128)(2,1)S(1)} %attend.7), channel_id=1, source_target_pairs={{0,64},{32,96},{64,0},{96,32},{1,65},{33,97},{65,1},{97,33},{2,66}... | collective-permute-start | bytes 983048 | tf_op jit(solution)/shard_map/ppermute | solution.py:232
  68.4 2.9 %attend.6 = s16[32,40,128]{2,1,0:T(8,128)(2,1)S(1)} custom-call(s32[2]{0:T(128)S(1)} %get-tuple-element.5.n_ref, bf16[32,2,16,128]{3,2,1,0:T(8,128)(2,1)S(1)} %collective-permute-done.5.q_ref, f32[32,128]{1,0:T(8,128)S(1)} %get-tuple-element.25.qm_ref, bf16[2,1152,256]{2,1,0:T(8,128)(2,1)S(1)} %get-tuple-element.14.k_ref, ...), custom_call_target="tpu_custom_call" | custom-call | flops 1207959552 | bytes 2359296 | tf_op jit(solution)/shard_map/attend/pallas_call | solution.py:185
  71.3 0.8 collective-permute-start.6
  72.1 2.8 %attend.5 = s16[32,40,128]{2,1,0:T(8,128)(2,1)S(1)} custom-call(s32[2]{0:T(128)S(1)} %get-tuple-element.5.n_ref, bf16[32,2,16,128]{3,2,1,0:T(8,128)(2,1)S(1)} %collective-permute-done.3.q_ref, f32[32,128]{1,0:T(8,128)S(1)} %get-tuple-element.24.qm_ref, bf16[2,1152,256]{2,1,0:T(8,128)(2,1)S(1)} %get-tuple-element.14.k_ref, ...), custom_call_target="tpu_custom_call" | custom-call | flops 1207959552 | bytes 2359296 | tf_op jit(solution)/shard_map/attend/pallas_call | solution.py:185
  74.9 1.1 collective-permute-start.4
  76.1 2.9 %attend.4.refs_0_ = s16[32,40,128]{2,1,0:T(8,128)(2,1)S(1)} custom-call(s32[2]{0:T(128)S(1)} %get-tuple-element.5.n_ref, bf16[32,2,16,128]{3,2,1,0:T(8,128)(2,1)S(1)} %all-to-all-done.q_ref, f32[32,128]{1,0:T(8,128)S(1)} %get-tuple-element.26.qm_ref, bf16[2,1152,256]{2,1,0:T(8,128)(2,1)S(1)} %get-tuple-element.14.k_ref, ...), custom_call_target="tpu_custom_call" | custom-call | flops 1207959552 | bytes 2359296 | tf_op jit(solution)/shard_map/attend/pallas_call | solution.py:185
  78.9 2.8 %collective-permute-done.6.refs_2_ = s16[32,40,128]{2,1,0:T(8,128)(2,1)S(1)} collective-permute-done((s16[32,40,128]{2,1,0:T(8,128)(2,1)S(1)}, s16[32,40,128]{2,1,0:T(8,128)(2,1)S(1)}, u32[]{:S(2)}, u32[]{:S(2)}) %collective-permute-start.6) | collective-permute-done | bytes 327712 | tf_op jit(solution)/shard_map/ppermute | solution.py:232
  81.7 1.0 collective-permute-done.4.refs_1_
  82.7 1.1 merge.1
  83.8 32.0 %all_to_all.10.p_ref = s16[32,40,128]{2,1,0:T(8,128)(2,1)S(1)} all-to-all(s16[32,40,128]{2,1,0:T(8,128)(2,1)S(1)} %merge.1), channel_id=1, replica_groups=mesh['groups'=2,'x'=4,'z'=16,'core'=2] {'z','core'}, dimensions={0} | all-to-all | bytes 655360 | tf_op jit(solution)/shard_map/all_to_all | solution.py:285
  115.9 0.3 finish.1
  116.2 0.6 copy.14
  (20 shorter events, 0.5 us)
Async XLA Ops:
  0.8 32.2 %collective-permute-start.1 = (bf16[2,256]{1,0:T(2,128)(2,1)S(1)}, bf16[2,256]{1,0:T(2,128)(2,1)S(1)}, u32[]{:S(2)}, u32[]{:S(2)}) collective-permute-start(bf16[2,256]{1,0:T(2,128)(2,1)S(1)} %get-tuple-element.16), channel_id=1, source_target_pairs={{0,1},{1,0},{2,3},{3,2},{4,5},{5,4},{6,7},{7,6},{8,9},{9,8},{10,11... | collective-permute-start | bytes 3080 | tf_op jit(solution)/shard_map/newer/ppermute | solution.py:256
  22.9 1.6 %copy-start = (bf16[1,8192]{1,0:T(2,128)(2,1)S(1)}, bf16[1,8192]{1,0:T(2,128)(2,1)}, u32[]{:S(2)}) copy-start(bf16[1,8192]{1,0:T(2,128)(2,1)} %param.7) | copy-start | bytes 49156
  22.9 8.3 %copy-start.1 = (s32[128]{0:T(128)S(1)}, s32[128]{0:T(128)}, u32[]{:S(2)}) copy-start(s32[128]{0:T(128)} %param.13) | copy-start | bytes 1540
  24.0 34.4 %collective-permute-start.2 = (bf16[2,1024,256]{2,1,0:T(8,128)(2,1)}, bf16[2,1024,256]{2,1,0:T(8,128)(2,1)S(1)}, u32[]{:S(2)}, u32[]{:S(2)}) collective-permute-start(bf16[2,1024,256]{2,1,0:T(8,128)(2,1)} %pad_maximum_fusion), channel_id=1, source_target_pairs={{0,1},{1,0},{2,3},{3,2},{4,5},{5,4},{6,7},{7,6},{8,9},{9,8},{10,11... | collective-permute-start | bytes 3145736 | tf_op jit(solution)/shard_map/swapped/ppermute | solution.py:253
  24.1 7.7 %collective-permute-start = (s32[1]{0:T(128)}, s32[1]{0:T(128)}, u32[]{:S(2)}, u32[]{:S(2)}) collective-permute-start(s32[1]{0:T(128)} %param.12), channel_id=1, source_target_pairs={{0,1},{1,0},{2,3},{3,2},{4,5},{5,4},{6,7},{7,6},{8,9},{9,8},{10,11... | collective-permute-start | bytes 20 | tf_op jit(solution)/shard_map/lengths/ppermute | solution.py:258
  25.4 27.3 %all-to-all-start = ((bf16[32,2,16,128]{3,2,1,0:T(8,128)(2,1)}), bf16[32,2,16,128]{3,2,1,0:T(8,128)(2,1)S(1)}, u32[]{:S(2)}, u32[]{:S(2)}) async-start(bf16[32,2,16,128]{3,2,1,0:T(8,128)(2,1)} %bitcast), calls=%async_computation | async-start | bytes 524288 | tf_op jit(solution)/shard_map/ask/all_to_all | solution.py:249
  52.7 8.9 %collective-permute-start.7 = (bf16[32,2,16,128]{3,2,1,0:T(8,128)(2,1)S(1)}, bf16[32,2,16,128]{3,2,1,0:T(8,128)(2,1)S(1)}, u32[]{:S(2)}, u32[]{:S(2)}) collective-permute-start(bf16[32,2,16,128]{3,2,1,0:T(8,128)(2,1)S(1)} %all-to-all-done.q_ref), channel_id=1, source_target_pairs={{0,64},{32,96},{64,0},{96,32},{1,65},{33,97},{65,1},{97,33},{2,66}... | collective-permute-start | bytes 786440 | tf_op jit(solution)/shard_map/ppermute | solution.py:232
  55.7 12.7 %collective-permute-start.5 = (bf16[32,2,16,128]{3,2,1,0:T(8,128)(2,1)S(1)}, bf16[32,2,16,128]{3,2,1,0:T(8,128)(2,1)S(1)}, u32[]{:S(2)}, u32[]{:S(2)}) collective-permute-start(bf16[32,2,16,128]{3,2,1,0:T(8,128)(2,1)S(1)} %all-to-all-done.q_ref), channel_id=1, source_target_pairs={{0,32},{32,64},{64,96},{96,0},{1,33},{33,65},{65,97},{97,1},{2,34}... | collective-permute-start | bytes 786440 | tf_op jit(solution)/shard_map/ppermute | solution.py:232
  56.2 15.9 %collective-permute-start.3 = (bf16[32,2,16,128]{3,2,1,0:T(8,128)(2,1)S(1)}, bf16[32,2,16,128]{3,2,1,0:T(8,128)(2,1)S(1)}, u32[]{:S(2)}, u32[]{:S(2)}) collective-permute-start(bf16[32,2,16,128]{3,2,1,0:T(8,128)(2,1)S(1)} %all-to-all-done.q_ref), channel_id=1, source_target_pairs={{0,96},{32,0},{64,32},{96,64},{1,97},{33,1},{65,33},{97,65},{2,98}... | collective-permute-start | bytes 786440 | tf_op jit(solution)/shard_map/ppermute | solution.py:232
  64.5 14.4 %collective-permute-start.8 = (s16[32,40,128]{2,1,0:T(8,128)(2,1)S(1)}, s16[32,40,128]{2,1,0:T(8,128)(2,1)S(1)}, u32[]{:S(2)}, u32[]{:S(2)}) collective-permute-start(s16[32,40,128]{2,1,0:T(8,128)(2,1)S(1)} %attend.7), channel_id=1, source_target_pairs={{0,64},{32,96},{64,0},{96,32},{1,65},{33,97},{65,1},{97,33},{2,66}... | collective-permute-start | bytes 983048 | tf_op jit(solution)/shard_map/ppermute | solution.py:232
  71.3 10.5 %collective-permute-start.6 = (s16[32,40,128]{2,1,0:T(8,128)(2,1)S(1)}, s16[32,40,128]{2,1,0:T(8,128)(2,1)S(1)}, u32[]{:S(2)}, u32[]{:S(2)}) collective-permute-start(s16[32,40,128]{2,1,0:T(8,128)(2,1)S(1)} %attend.6), channel_id=1, source_target_pairs={{0,96},{32,0},{64,32},{96,64},{1,97},{33,1},{65,33},{97,65},{2,98}... | collective-permute-start | bytes 983048 | tf_op jit(solution)/shard_map/ppermute | solution.py:232
  74.9 7.8 %collective-permute-start.4 = (s16[32,40,128]{2,1,0:T(8,128)(2,1)S(1)}, s16[32,40,128]{2,1,0:T(8,128)(2,1)S(1)}, u32[]{:S(2)}, u32[]{:S(2)}) collective-permute-start(s16[32,40,128]{2,1,0:T(8,128)(2,1)S(1)} %attend.5), channel_id=1, source_target_pairs={{0,32},{32,64},{64,96},{96,0},{1,33},{33,65},{65,97},{97,1},{2,34}... | collective-permute-start | bytes 983048 | tf_op jit(solution)/shard_map/ppermute | solution.py:232

commit v3 on v2

--- a/solution.py
+++ b/solution.py
@@ -8,6 +8,7 @@
 from jax.experimental.pallas import tpu as pltpu
 from jax.sharding import Mesh
 from jax.sharding import PartitionSpec as P
+
 
 HEADS_PER_GROUP = 16
 HEAD_WIDTH = 128
@@ -37,45 +38,47 @@
     return lax.rem(lane, rows) == row
 
 
-def attend_kernel(n_ref, q_ref, qm_ref, k_ref, km_ref, v_ref, o_ref, qa_scr, s_scr, m_scr, acc_scr, st_scr):
-    tokens, kv_heads, group, width = q_ref.shape
+def attend_kernel(pieces, n_ref, k_ref, km_ref, v_ref, *refs):
+    q_refs, qm_refs, o_refs = refs[:pieces], refs[pieces : 2 * pieces], refs[2 * pieces : 3 * pieces]
+    qa_scr, s_scr, m_scr, acc_scr, st_scr = refs[3 * pieces :]
+    tokens, kv_heads, group, width = q_refs[0].shape
     rows = tokens * group
+    chunks = o_refs[0].shape[0]
+    per = rows // chunks
     tile = rows // 2
-    chunks = o_ref.shape[0]
-    per = rows // chunks
-    units = [(kv, slice(r, r + tile)) for kv in range(kv_heads) for r in range(0, rows, tile)]
-
-    for kv in range(kv_heads):
-        qa_scr[kv, :, :width] = q_ref[:, kv].reshape(rows, width)
-        mask = jnp.broadcast_to(qm_ref[...][:, None, :], (tokens, group, 128))
-        qa_scr[kv, :, width:] = mask.reshape(rows, 128).astype(BF16)
+    blocks = [(p, kv) for p in range(pieces) for kv in range(kv_heads)]
+    units = [(h, kv, slice(r, r + tile)) for h, (p, kv) in enumerate(blocks) for r in range(0, rows, tile)]
+
+    for h, (p, kv) in enumerate(blocks):
+        qa_scr[h, :, :width] = q_refs[p][:, kv].reshape(rows, width)
+        mask = jnp.broadcast_to(qm_refs[p][...][:, None, :], (tokens, group, 128))
+        qa_scr[h, :, width:] = mask.reshape(rows, 128).astype(BF16)
 
     @pl.loop(0, 2)
     def block(blk):
         def variant(slots):
             spans = [slice(c, min(c + CHUNK, slots)) for c in range(0, slots, CHUNK)]
-            tops = []
-            for kv, r in units:
+            for h, kv, r in units:
                 top = None
                 for span in spans:
                     head = slice(kv * width, (kv + 1) * width)
                     k = jnp.concatenate([k_ref[blk, span, head], km_ref[blk, span, :]], axis=1)
-                    s = dot_nt(qa_scr[kv, r], k)
-                    s_scr[kv, r, span] = s
+                    s = dot_nt(qa_scr[h, r], k)
+                    s_scr[h, r, span] = s
                     for l in range(0, s.shape[1], 128):
                         part = s[:, l : l + 128]
                         top = part if top is None else jnp.maximum(top, part)
-                m_scr[blk, kv, r] = top
-            for kv, r in units:
-                top = jnp.max(m_scr[blk, kv, r], axis=1, keepdims=True)
+                m_scr[blk, h, r] = top
+            for h, kv, r in units:
+                top = jnp.max(m_scr[blk, h, r], axis=1, keepdims=True)
                 acc = None
                 for span in spans:
-                    p = jnp.exp2((s_scr[kv, r, span] - top) * LOG2_SCALE).astype(BF16)
+                    p = jnp.exp2((s_scr[h, r, span] - top) * LOG2_SCALE).astype(BF16)
                     v = v_ref[blk, span, kv * width : (kv + 1) * width]
                     term = dot_nn(p, jnp.concatenate([v, jnp.ones_like(v)], axis=1))
                     acc = term if acc is None else acc + term
-                acc_scr[blk, kv, r] = acc
-                m_scr[blk, kv, r] = jnp.broadcast_to(top * LOG2_SCALE, (tile, 128))
+                acc_scr[blk, h, r] = acc
+                m_scr[blk, h, r] = jnp.broadcast_to(top * LOG2_SCALE, (tile, 128))
 
         used, low = n_ref[blk], 0
         full = k_ref.shape[1]
@@ -83,25 +86,28 @@
             pl.when(jnp.logical_and(used > low, used <= slots))(functools.partial(variant, slots))
             low = slots
 
-    @pl.loop(0, kv_heads)
-    def close(kv):
-        m_a, m_b = m_scr[0, kv], m_scr[1, kv]
-        top = jnp.maximum(m_a, m_b)
-        w_a, w_b = jnp.exp2(m_a - top), jnp.exp2(m_b - top)
-        total = acc_scr[0, kv, :, width:] * w_a + acc_scr[1, kv, :, width:] * w_b
-        mean = (acc_scr[0, kv, :, :width] * w_a + acc_scr[1, kv, :, :width] * w_b) / total
-        lse = top + jnp.log2(total)
-        at = pl.multiple_of(kv * per, per)
-        coded, exponent = encode(mean)
-        o_ref[:, pl.ds(at, per), :] = coded.reshape(chunks, per, width).astype(I16)
-        pick = diagonal(per)[None]
-        st_scr[0, kv] = jnp.sum(jnp.where(pick, lse.reshape(chunks, per, 128), 0.0), axis=1)
-        spread = jnp.broadcast_to(exponent, (rows, 128)).reshape(chunks, per, 128)
-        st_scr[1, kv] = jnp.sum(jnp.where(pick, spread, 0.0), axis=1)
-
-    o_ref[:, kv_heads * per :, :] = stat_rows(
-        [st_scr[0, kv] for kv in range(kv_heads)], [st_scr[1, kv] for kv in range(kv_heads)]
-    )
+    for p in range(pieces):
+
+        @pl.loop(0, kv_heads)
+        def close(kv, p=p):
+            h = p * kv_heads + kv
+            m_a, m_b = m_scr[0, h], m_scr[1, h]
+            top = jnp.maximum(m_a, m_b)
+            w_a, w_b = jnp.exp2(m_a - top), jnp.exp2(m_b - top)
+            total = acc_scr[0, h, :, width:] * w_a + acc_scr[1, h, :, width:] * w_b
+            mean = (acc_scr[0, h, :, :width] * w_a + acc_scr[1, h, :, :width] * w_b) / total
+            lse = top + jnp.log2(total)
+            at = pl.multiple_of(kv * per, per)
+            coded, exponent = encode(mean)
+            o_refs[p][:, pl.ds(at, per), :] = coded.reshape(chunks, per, width).astype(I16)
+            pick = diagonal(per)[None]
+            st_scr[0, kv] = jnp.sum(jnp.where(pick, lse.reshape(chunks, per, 128), 0.0), axis=1)
+            spread = jnp.broadcast_to(exponent, (rows, 128)).reshape(chunks, per, 128)
+            st_scr[1, kv] = jnp.sum(jnp.where(pick, spread, 0.0), axis=1)
+
+        o_refs[p][:, kv_heads * per :, :] = stat_rows(
+            [st_scr[0, kv] for kv in range(kv_heads)], [st_scr[1, kv] for kv in range(kv_heads)]
+        )
 
 
 def encode(mean):
@@ -161,47 +167,52 @@
         o_ref[here, rows:, :] = stat_rows([lse[:, kv] for kv in range(2)], [exponents[:, kv] for kv in range(2)])
 
 
-def final_kernel(p_ref, o_ref):
-    sources, rows, width = p_ref.shape
-    rows -= STAT_ROWS
+def final_kernel(core_ref, p_ref, own_ref, other_ref, scr):
+    rows = p_ref.shape[1] - STAT_ROWS
+    group = rows // 4
     lse, scale = read_stats(p_ref[:, rows:, :])
-    lse = lse.reshape(sources // 2, 2, *lse.shape[1:])
     top = jnp.max(lse, axis=0, keepdims=True)
     weights = jnp.exp2(lse - top)
     weights = weights / jnp.sum(weights, axis=0, keepdims=True)
-    column = as_column(weights.reshape(scale.shape) * scale, rows // 2)
-    terms = (numbers(p_ref[:, :rows, :]) * column).reshape(sources // 2, 2 * rows, width)
-    o_ref[...] = jnp.sum(terms, axis=0).astype(BF16)
+    column = as_column(weights * scale, rows // 2)
+    out = jnp.sum(numbers(p_ref[:, :rows, :]) * column, axis=0).astype(BF16)
+    for kv in range(2):
+        for token in range(2):
+            at = (2 * kv + token) * group
+            scr[token, kv * group : (kv + 1) * group] = out[at : at + group]
+    own_ref[...] = scr[core_ref[0]]
+    other_ref[...] = scr[1 - core_ref[0]]
 
 
 VMEM_SPEC = pl.BlockSpec(memory_space=pltpu.VMEM)
 
 
-def attend(counts, q, q_mask, keys, key_mask, values):
-    tokens, kv_heads, group, width = q.shape
+def attend(counts, qs, q_masks, keys, key_mask, values):
+    tokens, kv_heads, group, width = qs[0].shape
     rows = tokens * group
     slots = keys.shape[1]
-    chunk_rows = kv_heads * group
+    pieces = len(qs)
+    out = jax.ShapeDtypeStruct((NZ, tokens // NZ * kv_heads * group + STAT_ROWS, width), I16)
     return pl.pallas_call(
-        attend_kernel,
-        out_shape=jax.ShapeDtypeStruct((tokens, chunk_rows + STAT_ROWS, width), I16),
-        in_specs=[pl.BlockSpec(memory_space=pltpu.SMEM)] + [VMEM_SPEC] * 5,
-        out_specs=VMEM_SPEC,
+        functools.partial(attend_kernel, pieces),
+        out_shape=[out] * pieces,
+        in_specs=[pl.BlockSpec(memory_space=pltpu.SMEM)] + [VMEM_SPEC] * (3 + 2 * pieces),
+        out_specs=[VMEM_SPEC] * pieces,
         scratch_shapes=[
-            pltpu.VMEM((kv_heads, rows, width + 128), BF16),
-            pltpu.VMEM((kv_heads, rows, slots), F32),
-            pltpu.VMEM((2, kv_heads, rows, 128), F32),
-            pltpu.VMEM((2, kv_heads, rows, 2 * width), F32),
-            pltpu.VMEM((2, kv_heads, tokens, 128), F32),
+            pltpu.VMEM((pieces * kv_heads, rows, width + 128), BF16),
+            pltpu.VMEM((pieces * kv_heads, rows, slots), F32),
+            pltpu.VMEM((2, pieces * kv_heads, rows, 128), F32),
+            pltpu.VMEM((2, pieces * kv_heads, rows, 2 * width), F32),
+            pltpu.VMEM((2, kv_heads, NZ, 128), F32),
         ],
         compiler_params=pltpu.CompilerParams(vmem_limit_bytes=32 * 1024 * 1024),
         cost_estimate=pl.CostEstimate(
-            flops=4 * rows * kv_heads * slots * 2 * width,
+            flops=4 * pieces * rows * kv_heads * slots * 2 * width,
             bytes_accessed=2 * (keys.size + values.size),
-            transcendentals=rows * kv_heads * slots,
+            transcendentals=pieces * rows * kv_heads * slots,
         ),
         name="attend",
-    )(counts, q, q_mask, keys, key_mask, values)
+    )(counts, keys, key_mask, values, *qs, *q_masks)
 
 
 def merge(pieces):
@@ -216,16 +227,18 @@
     )(*pieces)
 
 
-def finish(pieces):
+def finish(core, pieces):
+    half = jax.ShapeDtypeStruct(((pieces.shape[1] - STAT_ROWS) // 2, HEAD_WIDTH), BF16)
     return pl.pallas_call(
         final_kernel,
-        out_shape=jax.ShapeDtypeStruct((2 * (pieces.shape[1] - STAT_ROWS), HEAD_WIDTH), BF16),
-        in_specs=[VMEM_SPEC],
-        out_specs=VMEM_SPEC,
+        out_shape=[half, half],
+        in_specs=[pl.BlockSpec(memory_space=pltpu.SMEM), VMEM_SPEC],
+        out_specs=[VMEM_SPEC, VMEM_SPEC],
+        scratch_shapes=[pltpu.VMEM((2, *half.shape), BF16)],
         compiler_params=pltpu.CompilerParams(vmem_limit_bytes=4 * 1024 * 1024),
         cost_estimate=pl.CostEstimate(flops=4 * pieces.size, bytes_accessed=2 * pieces.size, transcendentals=0),
         name="finish",
-    )(pieces)
+    )(core.reshape(1), pieces)
 
 
 def along_x(a, step):
@@ -243,19 +256,15 @@
         size = a.shape[1] // 2
         return lax.dynamic_slice_in_dim(a, which * size, size, 1)
 
-    with jax.named_scope("ask"):
-        split = queries.reshape(1, 2, kv_mine, group, width)
-        split = jnp.broadcast_to(split, (NZ, *split.shape[1:])).reshape(NZ * 2, kv_mine, group, width)
-        column = lax.all_to_all(split, ("z", "core"), 0, 0, tiled=True)
-
-    with jax.named_scope("swapped"):
-        given = jnp.stack([half(cache_keys, 1 - core), half(stored_values, 1 - core)])
-        kv_got = lax.ppermute(given, "core", SWAP)
-    with jax.named_scope("newer"):
-        fresh = jnp.concatenate([fresh_keys, fresh_values], axis=0)
-        new = jnp.stack([half(fresh, core), lax.ppermute(half(fresh, 1 - core), "core", SWAP)])
-    with jax.named_scope("lengths"):
-        lengths = jnp.concatenate([cache_lengths, lax.ppermute(cache_lengths, "core", SWAP)])
+    split = queries.reshape(1, 2, kv_mine, group, width)
+    split = jnp.broadcast_to(split, (NZ, *split.shape[1:])).reshape(NZ * 2, kv_mine, group, width)
+    column = lax.all_to_all(split, ("z", "core"), 0, 0, tiled=True)
+
+    given = jnp.stack([half(cache_keys, 1 - core), half(stored_values, 1 - core)])
+    kv_got = lax.ppermute(given, "core", SWAP)
+    fresh = jnp.concatenate([fresh_keys, fresh_values], axis=0)
+    new = jnp.stack([half(fresh, core), lax.ppermute(half(fresh, 1 - core), "core", SWAP)])
+    lengths = jnp.concatenate([cache_lengths, lax.ppermute(cache_lengths, "core", SWAP)])
     slot = jnp.arange(padded, dtype=I32)
 
     def extended(own, other, added):
@@ -278,12 +287,18 @@
         there = lax.dynamic_slice(table, (lax.rem(x + step, NX), 0), (1, NZ * 2)).reshape(NZ * 2, 1)
         return jnp.where((lane[None, :] > there) | (lane[None, :] == 0), 1.0, 0.0).astype(F32)
 
-    steps = (0, 1, 3, 2)
-    asked = [column if s == 0 else along_x(column, s) for s in steps]
-    results = [attend(counts, q, q_mask(s), keys, key_mask, values) for q, s in zip(asked, steps)]
-    pieces = [r if s == 0 else along_x(r, -s) for r, s in zip(results, steps)]
-    merged = lax.all_to_all(merge(pieces), ("z", "core"), 0, 0, tiled=True)
-    return finish(merged).reshape(1, -1)
+    def results(*steps):
+        asked = [column if s == 0 else along_x(column, s) for s in steps]
+        return attend(counts, asked, [q_mask(s) for s in steps], keys, key_mask, values)
+
+    next_to, before = results(1, NX - 1)
+    (across,) = results(NX // 2)
+    (own,) = results(0)
+    merged = merge([own, along_x(next_to, -1), along_x(before, 1), along_x(across, -(NX // 2))])
+    mine, other = finish(core, lax.all_to_all(merged, "z", 0, 0, tiled=True))
+    back = lax.ppermute(other, "core", SWAP)
+    first, second = jnp.where(core == 0, mine, back), jnp.where(core == 0, back, mine)
+    return jnp.concatenate([first, second], axis=0).reshape(1, -1)
 
 
 def solution(mesh):

time: 117 us -> 110 us (0.940)
  blocking collectives: 32 us -> 16.5 us
  starting transfers between devices: 37.7 us -> 46 us
  Pallas kernels: 12.8 us -> 9.89 us
  waiting for transfers between devices: 25.6 us -> 27.7 us
    all_to_all x1, blocking collectives: 32 us -> 16.5 us  [body(): mine, other = finish(core, lax.all_to_all(merged, 'z', 0, 0, tiled=True))]
    ppermute x0 -> x1, starting transfers between devices: none -> 7.93 us  [body(): back = lax.ppermute(other, 'core', SWAP)]
    pallas_call x5 -> x4, Pallas kernels: 11.7 us -> 8.95 us  [the longest x3 8.68 us: attend(): pl.pallas_call(functools.partial(attend_kernel, pieces), out_shape=[out]...]
    ppermute x6, waiting for transfers between devices: 5.97 us -> 7.32 us  [along_x(): return lax.ppermute(a, 'x', [(i, (i - step) % NX) for i in range(NX)])]
  transfers between devices with their start and end apart: 10 -> 11, of which waited for: 4 -> 6; matrix products, arithmetic and copies ran while one was open for 5% -> 6% of each run, Pallas kernels for 10% -> 8%
where the time goes in v3:
time: 110 us; the launch traced here: 109 us
  starting transfers between devices  46 us (42%)
  waiting for transfers between devices  27.7 us (25%)
  blocking collectives  16.5 us (15%)
  Pallas kernels  9.89 us (9%)
  other arithmetic  4.5 us (4%)
  local copies, waits for them, and re-layouts  3.39 us (3%)
    ppermute x1, starting transfers between devices, body(): lax.ppermute(half(fresh, 1 - core), 'core', SWAP)  20.5 us
    all_to_all x1, waiting for transfers between devices, body(): column = lax.all_to_all(split, ('z', 'core'), 0, 0, tiled=True)  19.5 us
    all_to_all x1, blocking collectives, body(): mine, other = finish(core, lax.all_to_all(merged, 'z', 0, 0, tiled=True))  16.5 us
    ppermute x6, starting transfers between devices, along_x(): return lax.ppermute(a, 'x', [(i, (i - step) % NX) for i in range(NX)])  11.9 us
    pallas_call x3, Pallas kernels, attend(): pl.pallas_call(functools.partial(attend_kernel, pieces), out_shape=[out]...  8.68 us
    ppermute x1, starting transfers between devices, body(): back = lax.ppermute(other, 'core', SWAP)  7.93 us
    ppermute x6, waiting for transfers between devices, along_x(): return lax.ppermute(a, 'x', [(i, (i - step) % NX) for i in range(NX)])  7.32 us
    all_to_all x1, starting transfers between devices, body(): column = lax.all_to_all(split, ('z', 'core'), 0, 0, tiled=True)  5.17 us
  transfers between devices with their start and end apart: 11, of which 6 were waited for; matrix products, arithmetic and copies ran while one was open for 6% of the time, Pallas kernels for 8%

profile of v3, /device:TPU:33, one launch (start us, length us, event | category | flops | bytes accessed | tf_op | source)
XLA Modules:
  0.0 108.8 jit_solution(7942642667684291506)
XLA Ops:
  0.0 0.8 fusion.18
  0.8 20.5 %collective-permute-start.1 = (bf16[2,256]{1,0:T(2,128)(2,1)S(1)}, bf16[2,256]{1,0:T(2,128)(2,1)S(1)}, u32[]{:S(2)}, u32[]{:S(2)}) collective-permute-start(bf16[2,256]{1,0:T(2,128)(2,1)S(1)} %get-tuple-element.26), channel_id=1, source_target_pairs={{0,1},{1,0},{2,3},{3,2},{4,5},{5,4},{6,7},{7,6},{8,9},{9,8},{10,11... | collective-permute-start | bytes 3080 | tf_op jit(solution)/shard_map/ppermute | solution.py:266
  21.3 1.7 %dynamic-slice_bitcast_fusion = (bf16[1,1024,256]{2,1,0:T(8,128)(2,1)S(1)}, bf16[1,1024,256]{2,1,0:T(8,128)(2,1)S(1)}, bf16[1,1024,256]{2,1,0:T(8,128)(2,1)S(1)}, bf16[1,1024,256]{2,1,0:T(8,128)(2,1)S(1)}) fusion(bf16[1024,512]{1,0:T(8,128)(2,1)} %param.11, s32[]{:T(128)S(6)} %select_n.93, s32[]{:T(128)S(6)} %select_n.94, bf16[1024,512]{1,0:T(8,128)(2,1)} %param.10), kind=kLoop, calls=%fused_computation.12 | loop fusion | bytes 4194312 | tf_op jit(solution)/shard_map/stack | solution.py:271
  23.0 1.1 pad_maximum_fusion
  24.1 0.5 collective-permute-start
  24.6 0.1 reduce
  24.6 0.7 broadcast_in_dim.110
  25.4 5.2 %all-to-all-start = ((bf16[32,2,16,128]{3,2,1,0:T(8,128)(2,1)}), bf16[32,2,16,128]{3,2,1,0:T(8,128)(2,1)S(1)}, u32[]{:S(2)}, u32[]{:S(2)}) async-start(bf16[32,2,16,128]{3,2,1,0:T(8,128)(2,1)} %bitcast.8), calls=%async_computation | async-start | bytes 524288 | tf_op jit(solution)/shard_map/all_to_all | solution.py:261
  31.4 0.1 rev.3
  31.7 0.7 broadcast_add_fusion
  32.5 0.5 select_convert_fusion.km_ref
  33.1 19.5 %all-to-all-done.refs_0_ = bf16[32,2,16,128]{3,2,1,0:T(8,128)(2,1)S(1)} async-done(((bf16[32,2,16,128]{3,2,1,0:T(8,128)(2,1)}), bf16[32,2,16,128]{3,2,1,0:T(8,128)(2,1)S(1)}, u32[]{:S(2)}, u32[]{:S(2)}) %all-to-all-start) | async-done | bytes 262176 | tf_op jit(solution)/shard_map/all_to_all | solution.py:261
  52.7 3.0 %collective-permute-start.7 = (bf16[32,2,16,128]{3,2,1,0:T(8,128)(2,1)S(1)}, bf16[32,2,16,128]{3,2,1,0:T(8,128)(2,1)S(1)}, u32[]{:S(2)}, u32[]{:S(2)}) collective-permute-start(bf16[32,2,16,128]{3,2,1,0:T(8,128)(2,1)S(1)} %all-to-all-done.refs_0_), channel_id=1, source_target_pairs={{0,64},{32,96},{64,0},{96,32},{1,65},{33,97},{65,1},{97,33},{2,66}... | collective-permute-start | bytes 786440 | tf_op jit(solution)/shard_map/ppermute | solution.py:245
  55.7 0.7 collective-permute-start.3
  56.4 0.7 collective-permute-start.4
  57.2 1.0 fusion.7
  58.2 3.4 %collective-permute-done.7.refs_0_ = bf16[32,2,16,128]{3,2,1,0:T(8,128)(2,1)S(1)} collective-permute-done((bf16[32,2,16,128]{3,2,1,0:T(8,128)(2,1)S(1)}, bf16[32,2,16,128]{3,2,1,0:T(8,128)(2,1)S(1)}, u32[]{:S(2)}, u32[]{:S(2)}) %collective-permute-start.7) | collective-permute-done | bytes 262176 | tf_op jit(solution)/shard_map/ppermute | solution.py:245
  61.6 2.5 %attend.5 = s16[16,72,128]{2,1,0:T(8,128)(2,1)S(1)} custom-call(s32[2]{0:T(128)S(1)} %get-tuple-element.13.n_ref, bf16[2,1152,256]{2,1,0:T(8,128)(2,1)S(1)} %get-tuple-element.24.k_ref, bf16[2,1152,128]{2,1,0:T(8,128)(2,1)S(1)} %select_convert_fusion.km_ref, bf16[2,1152,256]{2,1,0:T(8,128)(2,1)S(1)} %get-tuple-element.23.v_ref, ...), custom_call_target="tpu_custom_call" | custom-call | flops 1207959552 | bytes 2359296 | tf_op jit(solution)/shard_map/attend/pallas_call | solution.py:196
  64.0 3.3 %collective-permute-start.8 = (s16[16,72,128]{2,1,0:T(8,128)(2,1)S(1)}, s16[16,72,128]{2,1,0:T(8,128)(2,1)S(1)}, u32[]{:S(2)}, u32[]{:S(2)}) collective-permute-start(s16[16,72,128]{2,1,0:T(8,128)(2,1)S(1)} %attend.5), channel_id=1, source_target_pairs={{0,64},{32,96},{64,0},{96,32},{1,65},{33,97},{65,1},{97,33},{2,66}... | collective-permute-start | bytes 884744 | tf_op jit(solution)/shard_map/ppermute | solution.py:245
  67.3 0.3 collective-permute-done.3.refs_0_
  67.6 0.4 collective-permute-done.4.refs_1_
  68.0 3.8 %attend.4 = (s16[16,72,128]{2,1,0:T(8,128)(2,1)S(1)}, s16[16,72,128]{2,1,0:T(8,128)(2,1)S(1)}) custom-call(s32[2]{0:T(128)S(1)} %get-tuple-element.13.n_ref, bf16[2,1152,256]{2,1,0:T(8,128)(2,1)S(1)} %get-tuple-element.24.k_ref, bf16[2,1152,128]{2,1,0:T(8,128)(2,1)S(1)} %select_convert_fusion.km_ref, bf16[2,1152,256]{2,1,0:T(8,128)(2,1)S(1)} %get-tuple-element.23.v_ref, ...), custom_call_target="tpu_custom_call" | custom-call | flops 2415919104 | bytes 2359296 | tf_op jit(solution)/shard_map/attend/pallas_call | solution.py:196
  71.8 2.3 %collective-permute-start.5 = (s16[16,72,128]{2,1,0:T(8,128)(2,1)S(1)}, s16[16,72,128]{2,1,0:T(8,128)(2,1)S(1)}, u32[]{:S(2)}, u32[]{:S(2)}) collective-permute-start(s16[16,72,128]{2,1,0:T(8,128)(2,1)S(1)} %get-tuple-element.9), channel_id=1, source_target_pairs={{0,32},{32,64},{64,96},{96,0},{1,33},{33,65},{65,97},{97,1},{2,34}... | collective-permute-start | bytes 884744 | tf_op jit(solution)/shard_map/ppermute | solution.py:245
  74.0 1.9 %collective-permute-start.6 = (s16[16,72,128]{2,1,0:T(8,128)(2,1)S(1)}, s16[16,72,128]{2,1,0:T(8,128)(2,1)S(1)}, u32[]{:S(2)}, u32[]{:S(2)}) collective-permute-start(s16[16,72,128]{2,1,0:T(8,128)(2,1)S(1)} %get-tuple-element.10), channel_id=1, source_target_pairs={{0,96},{32,0},{64,32},{96,64},{1,97},{33,1},{65,33},{97,65},{2,98}... | collective-permute-start | bytes 884744 | tf_op jit(solution)/shard_map/ppermute | solution.py:245
  75.9 2.5 %attend.3.refs_0_ = s16[16,72,128]{2,1,0:T(8,128)(2,1)S(1)} custom-call(s32[2]{0:T(128)S(1)} %get-tuple-element.13.n_ref, bf16[2,1152,256]{2,1,0:T(8,128)(2,1)S(1)} %get-tuple-element.24.k_ref, bf16[2,1152,128]{2,1,0:T(8,128)(2,1)S(1)} %select_convert_fusion.km_ref, bf16[2,1152,256]{2,1,0:T(8,128)(2,1)S(1)} %get-tuple-element.23.v_ref, ...), custom_call_target="tpu_custom_call" | custom-call | flops 1207959552 | bytes 2359296 | tf_op jit(solution)/shard_map/attend/pallas_call | solution.py:196
  78.4 3.3 %collective-permute-done.5.refs_1_ = s16[16,72,128]{2,1,0:T(8,128)(2,1)S(1)} collective-permute-done((s16[16,72,128]{2,1,0:T(8,128)(2,1)S(1)}, s16[16,72,128]{2,1,0:T(8,128)(2,1)S(1)}, u32[]{:S(2)}, u32[]{:S(2)}) %collective-permute-start.5) | collective-permute-done | bytes 294944 | tf_op jit(solution)/shard_map/ppermute | solution.py:245
  81.6 0.9 merge.1
  82.6 16.5 %all_to_all.10.p_ref = s16[16,72,128]{2,1,0:T(8,128)(2,1)S(1)} all-to-all(s16[16,72,128]{2,1,0:T(8,128)(2,1)S(1)} %merge.1), channel_id=1, replica_groups=mesh['groups'=2,'x'=4,'z'=16,'core'=2] {'z'}, dimensions={0} | all-to-all | bytes 589824 | tf_op jit(solution)/shard_map/all_to_all | solution.py:298
  99.1 0.3 finish.1
  99.4 7.9 %collective-permute-start.9 = (bf16[32,128]{1,0:T(8,128)(2,1)S(1)}, bf16[32,128]{1,0:T(8,128)(2,1)S(1)}, u32[]{:S(2)}, u32[]{:S(2)}) collective-permute-start(bf16[32,128]{1,0:T(8,128)(2,1)S(1)} %get-tuple-element.12), channel_id=1, source_target_pairs={{0,1},{1,0},{2,3},{3,2},{4,5},{5,4},{6,7},{7,6},{8,9},{9,8},{10,11... | collective-permute-start | bytes 24584 | tf_op jit(solution)/shard_map/ppermute | solution.py:299
  107.3 0.8 collective-permute-done.9
  108.2 0.6 copy.14
  (23 shorter events, 0.7 us)
Async XLA Ops:
  0.8 32.3 %collective-permute-start.1 = (bf16[2,256]{1,0:T(2,128)(2,1)S(1)}, bf16[2,256]{1,0:T(2,128)(2,1)S(1)}, u32[]{:S(2)}, u32[]{:S(2)}) collective-permute-start(bf16[2,256]{1,0:T(2,128)(2,1)S(1)} %get-tuple-element.26), channel_id=1, source_target_pairs={{0,1},{1,0},{2,3},{3,2},{4,5},{5,4},{6,7},{7,6},{8,9},{9,8},{10,11... | collective-permute-start | bytes 3080 | tf_op jit(solution)/shard_map/ppermute | solution.py:266
  22.9 1.6 %copy-start = (bf16[1,8192]{1,0:T(2,128)(2,1)S(1)}, bf16[1,8192]{1,0:T(2,128)(2,1)}, u32[]{:S(2)}) copy-start(bf16[1,8192]{1,0:T(2,128)(2,1)} %param.7) | copy-start | bytes 49156
  22.9 8.3 %copy-start.1 = (s32[128]{0:T(128)S(1)}, s32[128]{0:T(128)}, u32[]{:S(2)}) copy-start(s32[128]{0:T(128)} %param.13) | copy-start | bytes 1540
  24.0 33.1 %collective-permute-start.2 = (bf16[2,1024,256]{2,1,0:T(8,128)(2,1)}, bf16[2,1024,256]{2,1,0:T(8,128)(2,1)S(1)}, u32[]{:S(2)}, u32[]{:S(2)}) collective-permute-start(bf16[2,1024,256]{2,1,0:T(8,128)(2,1)} %pad_maximum_fusion), channel_id=1, source_target_pairs={{0,1},{1,0},{2,3},{3,2},{4,5},{5,4},{6,7},{7,6},{8,9},{9,8},{10,11... | collective-permute-start | bytes 3145736 | tf_op jit(solution)/shard_map/ppermute | solution.py:264
  24.1 7.6 %collective-permute-start = (s32[1]{0:T(128)}, s32[1]{0:T(128)}, u32[]{:S(2)}, u32[]{:S(2)}) collective-permute-start(s32[1]{0:T(128)} %param.12), channel_id=1, source_target_pairs={{0,1},{1,0},{2,3},{3,2},{4,5},{5,4},{6,7},{7,6},{8,9},{9,8},{10,11... | collective-permute-start | bytes 20 | tf_op jit(solution)/shard_map/ppermute | solution.py:267
  25.4 27.3 %all-to-all-start = ((bf16[32,2,16,128]{3,2,1,0:T(8,128)(2,1)}), bf16[32,2,16,128]{3,2,1,0:T(8,128)(2,1)S(1)}, u32[]{:S(2)}, u32[]{:S(2)}) async-start(bf16[32,2,16,128]{3,2,1,0:T(8,128)(2,1)} %bitcast.8), calls=%async_computation | async-start | bytes 524288 | tf_op jit(solution)/shard_map/all_to_all | solution.py:261
  52.7 8.9 %collective-permute-start.7 = (bf16[32,2,16,128]{3,2,1,0:T(8,128)(2,1)S(1)}, bf16[32,2,16,128]{3,2,1,0:T(8,128)(2,1)S(1)}, u32[]{:S(2)}, u32[]{:S(2)}) collective-permute-start(bf16[32,2,16,128]{3,2,1,0:T(8,128)(2,1)S(1)} %all-to-all-done.refs_0_), channel_id=1, source_target_pairs={{0,64},{32,96},{64,0},{96,32},{1,65},{33,97},{65,1},{97,33},{2,66}... | collective-permute-start | bytes 786440 | tf_op jit(solution)/shard_map/ppermute | solution.py:245
  55.7 11.9 %collective-permute-start.3 = (bf16[32,2,16,128]{3,2,1,0:T(8,128)(2,1)S(1)}, bf16[32,2,16,128]{3,2,1,0:T(8,128)(2,1)S(1)}, u32[]{:S(2)}, u32[]{:S(2)}) collective-permute-start(bf16[32,2,16,128]{3,2,1,0:T(8,128)(2,1)S(1)} %all-to-all-done.refs_0_), channel_id=1, source_target_pairs={{0,96},{32,0},{64,32},{96,64},{1,97},{33,1},{65,33},{97,65},{2,98}... | collective-permute-start | bytes 786440 | tf_op jit(solution)/shard_map/ppermute | solution.py:245
  56.4 11.6 %collective-permute-start.4 = (bf16[32,2,16,128]{3,2,1,0:T(8,128)(2,1)S(1)}, bf16[32,2,16,128]{3,2,1,0:T(8,128)(2,1)S(1)}, u32[]{:S(2)}, u32[]{:S(2)}) collective-permute-start(bf16[32,2,16,128]{3,2,1,0:T(8,128)(2,1)S(1)} %all-to-all-done.refs_0_), channel_id=1, source_target_pairs={{0,32},{32,64},{64,96},{96,0},{1,33},{33,65},{65,97},{97,1},{2,34}... | collective-permute-start | bytes 786440 | tf_op jit(solution)/shard_map/ppermute | solution.py:245
  64.0 14.3 %collective-permute-start.8 = (s16[16,72,128]{2,1,0:T(8,128)(2,1)S(1)}, s16[16,72,128]{2,1,0:T(8,128)(2,1)S(1)}, u32[]{:S(2)}, u32[]{:S(2)}) collective-permute-start(s16[16,72,128]{2,1,0:T(8,128)(2,1)S(1)} %attend.5), channel_id=1, source_target_pairs={{0,64},{32,96},{64,0},{96,32},{1,65},{33,97},{65,1},{97,33},{2,66}... | collective-permute-start | bytes 884744 | tf_op jit(solution)/shard_map/ppermute | solution.py:245
  71.8 9.9 %collective-permute-start.5 = (s16[16,72,128]{2,1,0:T(8,128)(2,1)S(1)}, s16[16,72,128]{2,1,0:T(8,128)(2,1)S(1)}, u32[]{:S(2)}, u32[]{:S(2)}) collective-permute-start(s16[16,72,128]{2,1,0:T(8,128)(2,1)S(1)} %get-tuple-element.9), channel_id=1, source_target_pairs={{0,32},{32,64},{64,96},{96,0},{1,33},{33,65},{65,97},{97,1},{2,34}... | collective-permute-start | bytes 884744 | tf_op jit(solution)/shard_map/ppermute | solution.py:245
  74.0 7.6 %collective-permute-start.6 = (s16[16,72,128]{2,1,0:T(8,128)(2,1)S(1)}, s16[16,72,128]{2,1,0:T(8,128)(2,1)S(1)}, u32[]{:S(2)}, u32[]{:S(2)}) collective-permute-start(s16[16,72,128]{2,1,0:T(8,128)(2,1)S(1)} %get-tuple-element.10), channel_id=1, source_target_pairs={{0,96},{32,0},{64,32},{96,64},{1,97},{33,1},{65,33},{97,65},{2,98}... | collective-permute-start | bytes 884744 | tf_op jit(solution)/shard_map/ppermute | solution.py:245
  99.4 8.8 %collective-permute-start.9 = (bf16[32,128]{1,0:T(8,128)(2,1)S(1)}, bf16[32,128]{1,0:T(8,128)(2,1)S(1)}, u32[]{:S(2)}, u32[]{:S(2)}) collective-permute-start(bf16[32,128]{1,0:T(8,128)(2,1)S(1)} %get-tuple-element.12), channel_id=1, source_target_pairs={{0,1},{1,0},{2,3},{3,2},{4,5},{5,4},{6,7},{7,6},{8,9},{9,8},{10,11... | collective-permute-start | bytes 24584 | tf_op jit(solution)/shard_map/ppermute | solution.py:299

commit v4 on v3

--- a/solution.py
+++ b/solution.py
@@ -287,14 +287,22 @@
         there = lax.dynamic_slice(table, (lax.rem(x + step, NX), 0), (1, NZ * 2)).reshape(NZ * 2, 1)
         return jnp.where((lane[None, :] > there) | (lane[None, :] == 0), 1.0, 0.0).astype(F32)
 
+    def fetched(step):
+        return along_x(column, step)
+
     def results(*steps):
-        asked = [column if s == 0 else along_x(column, s) for s in steps]
+        asked = [column if s == 0 else fetched(s) for s in steps]
         return attend(counts, asked, [q_mask(s) for s in steps], keys, key_mask, values)
 
-    next_to, before = results(1, NX - 1)
+    (next_to,) = results(1)
+    (before,) = results(NX - 1)
     (across,) = results(NX // 2)
     (own,) = results(0)
-    merged = merge([own, along_x(next_to, -1), along_x(before, 1), along_x(across, -(NX // 2))])
+
+    def returned(a, step):
+        return along_x(a, -step)
+
+    merged = merge([own, returned(next_to, 1), returned(before, NX - 1), returned(across, NX // 2)])
     mine, other = finish(core, lax.all_to_all(merged, "z", 0, 0, tiled=True))
     back = lax.ppermute(other, "core", SWAP)
     first, second = jnp.where(core == 0, mine, back), jnp.where(core == 0, back, mine)

time: 110 us -> 115 us (1.045)
  waiting for transfers between devices: 27.7 us -> 33.3 us
  starting transfers between devices: 46 us -> 44.3 us
    ppermute x1, starting transfers between devices: 0.47 us -> 20.4 us  [body(): lax.ppermute(cache_lengths, 'core', SWAP)]
    ppermute x1, starting transfers between devices: 20.5 us -> 0.56 us  [body(): lax.ppermute(half(fresh, 1 - core), 'core', SWAP)]
    ppermute x6, waiting for transfers between devices: 7.32 us -> 12.9 us  [along_x(): return lax.ppermute(a, 'x', [(i, (i - step) % NX) for i in range(NX)])]
    ppermute x6, starting transfers between devices: 11.9 us -> 10.3 us  [along_x(): return lax.ppermute(a, 'x', [(i, (i - step) % NX) for i in range(NX)])]
    pallas_call x3 -> x4, Pallas kernels: 8.68 us -> 9.81 us  [attend(): pl.pallas_call(functools.partial(attend_kernel, pieces), out_shape=[out]...]
  transfers between devices with their start and end apart: 11 -> 11, of which waited for: 6 -> 4; matrix products, arithmetic and copies ran while one was open for 6% -> 6% of each run, Pallas kernels for 8% -> 9%
where the time goes in v4:
time: 115 us; the launch traced here: 113 us
  starting transfers between devices  44.3 us (39%)
  waiting for transfers between devices  33.3 us (29%)
  blocking collectives  16.8 us (15%)
  Pallas kernels  11 us (10%)
  other arithmetic  3.82 us (3%)
  local copies, waits for them, and re-layouts  3.41 us (3%)
    ppermute x1, starting transfers between devices, body(): lax.ppermute(cache_lengths, 'core', SWAP)  20.4 us
    all_to_all x1, waiting for transfers between devices, body(): column = lax.all_to_all(split, ('z', 'core'), 0, 0, tiled=True)  19.5 us
    all_to_all x1, blocking collectives, body(): mine, other = finish(core, lax.all_to_all(merged, 'z', 0, 0, tiled=True))  16.8 us
    ppermute x6, waiting for transfers between devices, along_x(): return lax.ppermute(a, 'x', [(i, (i - step) % NX) for i in range(NX)])  12.9 us
    ppermute x6, starting transfers between devices, along_x(): return lax.ppermute(a, 'x', [(i, (i - step) % NX) for i in range(NX)])  10.3 us
    pallas_call x4, Pallas kernels, attend(): pl.pallas_call(functools.partial(attend_kernel, pieces), out_shape=[out]...  9.81 us
    ppermute x1, starting transfers between devices, body(): back = lax.ppermute(other, 'core', SWAP)  7.81 us
    all_to_all x1, starting transfers between devices, body(): column = lax.all_to_all(split, ('z', 'core'), 0, 0, tiled=True)  5.17 us
  transfers between devices with their start and end apart: 11, of which 4 were waited for; matrix products, arithmetic and copies ran while one was open for 6% of the time, Pallas kernels for 9%

profile of v4, /device:TPU:33, one launch (start us, length us, event | category | flops | bytes accessed | tf_op | source)
XLA Modules:
  0.0 113.4 jit_solution(6674515585248412348)
XLA Ops:
  0.0 20.4 %collective-permute-start = (s32[1]{0:T(128)}, s32[1]{0:T(128)}, u32[]{:S(2)}, u32[]{:S(2)}) collective-permute-start(s32[1]{0:T(128)} %param.12), channel_id=1, source_target_pairs={{0,1},{1,0},{2,3},{3,2},{4,5},{5,4},{6,7},{7,6},{8,9},{9,8},{10,11... | collective-permute-start | bytes 20 | tf_op jit(solution)/shard_map/ppermute | solution.py:267
  20.4 1.7 %dynamic-slice_bitcast_fusion = (bf16[1,1024,256]{2,1,0:T(8,128)(2,1)S(1)}, bf16[1,1024,256]{2,1,0:T(8,128)(2,1)S(1)}, bf16[1,1024,256]{2,1,0:T(8,128)(2,1)S(1)}, bf16[1,1024,256]{2,1,0:T(8,128)(2,1)S(1)}) fusion(bf16[1024,512]{1,0:T(8,128)(2,1)} %param.11, s32[]{:T(128)S(6)} %select_n.93, s32[]{:T(128)S(6)} %select_n.94, bf16[1024,512]{1,0:T(8,128)(2,1)} %param.10), kind=kLoop, calls=%fused_computation.12 | loop fusion | bytes 4194312 | tf_op jit(solution)/shard_map/stack | solution.py:271
  22.1 1.1 pad_maximum_fusion
  23.2 0.1 fusion.18
  23.3 0.6 collective-permute-start.1
  23.9 0.1 reduce
  24.0 0.8 broadcast_in_dim.110
  24.7 5.2 %all-to-all-start = ((bf16[32,2,16,128]{3,2,1,0:T(8,128)(2,1)}), bf16[32,2,16,128]{3,2,1,0:T(8,128)(2,1)S(1)}, u32[]{:S(2)}, u32[]{:S(2)}) async-start(bf16[32,2,16,128]{3,2,1,0:T(8,128)(2,1)} %bitcast.8), calls=%async_computation | async-start | bytes 524288 | tf_op jit(solution)/shard_map/all_to_all | solution.py:261
  30.6 0.1 reshape.105
  30.7 0.1 rev.3
  30.9 0.1 fusion.15
  31.0 0.8 broadcast_add_fusion
  31.9 0.5 select_convert_fusion.km_ref
  32.5 19.5 %all-to-all-done.refs_0_ = bf16[32,2,16,128]{3,2,1,0:T(8,128)(2,1)S(1)} async-done(((bf16[32,2,16,128]{3,2,1,0:T(8,128)(2,1)}), bf16[32,2,16,128]{3,2,1,0:T(8,128)(2,1)S(1)}, u32[]{:S(2)}, u32[]{:S(2)}) %all-to-all-start) | async-done | bytes 262176 | tf_op jit(solution)/shard_map/all_to_all | solution.py:261
  52.0 2.9 %collective-permute-start.3 = (bf16[32,2,16,128]{3,2,1,0:T(8,128)(2,1)S(1)}, bf16[32,2,16,128]{3,2,1,0:T(8,128)(2,1)S(1)}, u32[]{:S(2)}, u32[]{:S(2)}) collective-permute-start(bf16[32,2,16,128]{3,2,1,0:T(8,128)(2,1)S(1)} %all-to-all-done.refs_0_), channel_id=1, source_target_pairs={{0,96},{32,0},{64,32},{96,64},{1,97},{33,1},{65,33},{97,65},{2,98}... | collective-permute-start | bytes 786440 | tf_op jit(solution)/shard_map/ppermute | solution.py:245
  54.9 1.6 %collective-permute-start.7 = (bf16[32,2,16,128]{3,2,1,0:T(8,128)(2,1)S(1)}, bf16[32,2,16,128]{3,2,1,0:T(8,128)(2,1)S(1)}, u32[]{:S(2)}, u32[]{:S(2)}) collective-permute-start(bf16[32,2,16,128]{3,2,1,0:T(8,128)(2,1)S(1)} %all-to-all-done.refs_0_), channel_id=1, source_target_pairs={{0,64},{32,96},{64,0},{96,32},{1,65},{33,97},{65,1},{97,33},{2,66}... | collective-permute-start | bytes 786440 | tf_op jit(solution)/shard_map/ppermute | solution.py:245
  56.6 1.0 fusion.7
  57.5 7.9 %collective-permute-done.3.refs_0_ = bf16[32,2,16,128]{3,2,1,0:T(8,128)(2,1)S(1)} collective-permute-done((bf16[32,2,16,128]{3,2,1,0:T(8,128)(2,1)S(1)}, bf16[32,2,16,128]{3,2,1,0:T(8,128)(2,1)S(1)}, u32[]{:S(2)}, u32[]{:S(2)}) %collective-permute-start.3) | collective-permute-done | bytes 262176 | tf_op jit(solution)/shard_map/ppermute | solution.py:245
  65.4 2.5 %attend.5 = s16[16,72,128]{2,1,0:T(8,128)(2,1)S(1)} custom-call(s32[2]{0:T(128)S(1)} %get-tuple-element.9.n_ref, bf16[2,1152,256]{2,1,0:T(8,128)(2,1)S(1)} %get-tuple-element.20.k_ref, bf16[2,1152,128]{2,1,0:T(8,128)(2,1)S(1)} %select_convert_fusion.km_ref, bf16[2,1152,256]{2,1,0:T(8,128)(2,1)S(1)} %get-tuple-element.19.v_ref, ...), custom_call_target="tpu_custom_call" | custom-call | flops 1207959552 | bytes 2359296 | tf_op jit(solution)/shard_map/attend/pallas_call | solution.py:196
  67.9 0.3 collective-permute-start.4
  68.2 2.5 %attend.6 = s16[16,72,128]{2,1,0:T(8,128)(2,1)S(1)} custom-call(s32[2]{0:T(128)S(1)} %get-tuple-element.9.n_ref, bf16[2,1152,256]{2,1,0:T(8,128)(2,1)S(1)} %get-tuple-element.20.k_ref, bf16[2,1152,128]{2,1,0:T(8,128)(2,1)S(1)} %select_convert_fusion.km_ref, bf16[2,1152,256]{2,1,0:T(8,128)(2,1)S(1)} %get-tuple-element.19.v_ref, ...), custom_call_target="tpu_custom_call" | custom-call | flops 1207959552 | bytes 2359296 | tf_op jit(solution)/shard_map/attend/pallas_call | solution.py:196
  70.7 4.3 %collective-permute-start.6 = (s16[16,72,128]{2,1,0:T(8,128)(2,1)S(1)}, s16[16,72,128]{2,1,0:T(8,128)(2,1)S(1)}, u32[]{:S(2)}, u32[]{:S(2)}) collective-permute-start(s16[16,72,128]{2,1,0:T(8,128)(2,1)S(1)} %attend.6), channel_id=1, source_target_pairs={{0,96},{32,0},{64,32},{96,64},{1,97},{33,1},{65,33},{97,65},{2,98}... | collective-permute-start | bytes 884744 | tf_op jit(solution)/shard_map/ppermute | solution.py:245
  75.0 2.5 %attend.7 = s16[16,72,128]{2,1,0:T(8,128)(2,1)S(1)} custom-call(s32[2]{0:T(128)S(1)} %get-tuple-element.9.n_ref, bf16[2,1152,256]{2,1,0:T(8,128)(2,1)S(1)} %get-tuple-element.20.k_ref, bf16[2,1152,128]{2,1,0:T(8,128)(2,1)S(1)} %select_convert_fusion.km_ref, bf16[2,1152,256]{2,1,0:T(8,128)(2,1)S(1)} %get-tuple-element.19.v_ref, ...), custom_call_target="tpu_custom_call" | custom-call | flops 1207959552 | bytes 2359296 | tf_op jit(solution)/shard_map/attend/pallas_call | solution.py:196
  77.4 1.2 %collective-permute-start.8 = (s16[16,72,128]{2,1,0:T(8,128)(2,1)S(1)}, s16[16,72,128]{2,1,0:T(8,128)(2,1)S(1)}, u32[]{:S(2)}, u32[]{:S(2)}) collective-permute-start(s16[16,72,128]{2,1,0:T(8,128)(2,1)S(1)} %attend.7), channel_id=1, source_target_pairs={{0,64},{32,96},{64,0},{96,32},{1,65},{33,97},{65,1},{97,33},{2,66}... | collective-permute-start | bytes 884744 | tf_op jit(solution)/shard_map/ppermute | solution.py:245
  78.7 2.5 %attend.4.refs_0_ = s16[16,72,128]{2,1,0:T(8,128)(2,1)S(1)} custom-call(s32[2]{0:T(128)S(1)} %get-tuple-element.9.n_ref, bf16[2,1152,256]{2,1,0:T(8,128)(2,1)S(1)} %get-tuple-element.20.k_ref, bf16[2,1152,128]{2,1,0:T(8,128)(2,1)S(1)} %select_convert_fusion.km_ref, bf16[2,1152,256]{2,1,0:T(8,128)(2,1)S(1)} %get-tuple-element.19.v_ref, ...), custom_call_target="tpu_custom_call" | custom-call | flops 1207959552 | bytes 2359296 | tf_op jit(solution)/shard_map/attend/pallas_call | solution.py:196
  81.1 5.0 %collective-permute-done.8.refs_3_ = s16[16,72,128]{2,1,0:T(8,128)(2,1)S(1)} collective-permute-done((s16[16,72,128]{2,1,0:T(8,128)(2,1)S(1)}, s16[16,72,128]{2,1,0:T(8,128)(2,1)S(1)}, u32[]{:S(2)}, u32[]{:S(2)}) %collective-permute-start.8) | collective-permute-done | bytes 294944 | tf_op jit(solution)/shard_map/ppermute | solution.py:245
  86.1 0.9 merge.1
  87.1 16.8 %all_to_all.10.p_ref = s16[16,72,128]{2,1,0:T(8,128)(2,1)S(1)} all-to-all(s16[16,72,128]{2,1,0:T(8,128)(2,1)S(1)} %merge.1), channel_id=1, replica_groups=mesh['groups'=2,'x'=4,'z'=16,'core'=2] {'z'}, dimensions={0} | all-to-all | bytes 589824 | tf_op jit(solution)/shard_map/all_to_all | solution.py:306
  103.9 0.3 finish.1
  104.1 7.8 %collective-permute-start.9 = (bf16[32,128]{1,0:T(8,128)(2,1)S(1)}, bf16[32,128]{1,0:T(8,128)(2,1)S(1)}, u32[]{:S(2)}, u32[]{:S(2)}) collective-permute-start(bf16[32,128]{1,0:T(8,128)(2,1)S(1)} %get-tuple-element.8), channel_id=1, source_target_pairs={{0,1},{1,0},{2,3},{3,2},{4,5},{5,4},{6,7},{7,6},{8,9},{9,8},{10,11... | collective-permute-start | bytes 24584 | tf_op jit(solution)/shard_map/ppermute | solution.py:307
  112.0 0.8 collective-permute-done.9
  112.8 0.6 copy.14
  (28 shorter events, 0.5 us)
Async XLA Ops:
  0.0 31.0 %collective-permute-start = (s32[1]{0:T(128)}, s32[1]{0:T(128)}, u32[]{:S(2)}, u32[]{:S(2)}) collective-permute-start(s32[1]{0:T(128)} %param.12), channel_id=1, source_target_pairs={{0,1},{1,0},{2,3},{3,2},{4,5},{5,4},{6,7},{7,6},{8,9},{9,8},{10,11... | collective-permute-start | bytes 20 | tf_op jit(solution)/shard_map/ppermute | solution.py:267
  22.1 1.1 %copy-start.1 = (bf16[1,512]{1,0:T(2,128)(2,1)S(1)}, bf16[1,512]{1,0:T(2,128)(2,1)}, u32[]{:S(2)}) copy-start(bf16[1,512]{1,0:T(2,128)(2,1)} %param.9) | copy-start | bytes 3076
  22.1 1.1 copy-start.2
  22.1 1.8 %copy-start = (bf16[1,8192]{1,0:T(2,128)(2,1)S(1)}, bf16[1,8192]{1,0:T(2,128)(2,1)}, u32[]{:S(2)}) copy-start(bf16[1,8192]{1,0:T(2,128)(2,1)} %param.7) | copy-start | bytes 49156
  22.1 8.5 %copy-start.3 = (s32[128]{0:T(128)S(1)}, s32[128]{0:T(128)}, u32[]{:S(2)}) copy-start(s32[128]{0:T(128)} %param.13) | copy-start | bytes 1540
  23.2 33.3 %collective-permute-start.2 = (bf16[2,1024,256]{2,1,0:T(8,128)(2,1)}, bf16[2,1024,256]{2,1,0:T(8,128)(2,1)S(1)}, u32[]{:S(2)}, u32[]{:S(2)}) collective-permute-start(bf16[2,1024,256]{2,1,0:T(8,128)(2,1)} %pad_maximum_fusion), channel_id=1, source_target_pairs={{0,1},{1,0},{2,3},{3,2},{4,5},{5,4},{6,7},{7,6},{8,9},{9,8},{10,11... | collective-permute-start | bytes 3145736 | tf_op jit(solution)/shard_map/ppermute | solution.py:264
  23.3 9.2 %collective-permute-start.1 = (bf16[2,256]{1,0:T(2,128)(2,1)S(1)}, bf16[2,256]{1,0:T(2,128)(2,1)S(1)}, u32[]{:S(2)}, u32[]{:S(2)}) collective-permute-start(bf16[2,256]{1,0:T(2,128)(2,1)S(1)} %get-tuple-element.22), channel_id=1, source_target_pairs={{0,1},{1,0},{2,3},{3,2},{4,5},{5,4},{6,7},{7,6},{8,9},{9,8},{10,11... | collective-permute-start | bytes 3080 | tf_op jit(solution)/shard_map/ppermute | solution.py:266
  24.7 27.3 %all-to-all-start = ((bf16[32,2,16,128]{3,2,1,0:T(8,128)(2,1)}), bf16[32,2,16,128]{3,2,1,0:T(8,128)(2,1)S(1)}, u32[]{:S(2)}, u32[]{:S(2)}) async-start(bf16[32,2,16,128]{3,2,1,0:T(8,128)(2,1)} %bitcast.8), calls=%async_computation | async-start | bytes 524288 | tf_op jit(solution)/shard_map/all_to_all | solution.py:261
  52.0 13.4 %collective-permute-start.3 = (bf16[32,2,16,128]{3,2,1,0:T(8,128)(2,1)S(1)}, bf16[32,2,16,128]{3,2,1,0:T(8,128)(2,1)S(1)}, u32[]{:S(2)}, u32[]{:S(2)}) collective-permute-start(bf16[32,2,16,128]{3,2,1,0:T(8,128)(2,1)S(1)} %all-to-all-done.refs_0_), channel_id=1, source_target_pairs={{0,96},{32,0},{64,32},{96,64},{1,97},{33,1},{65,33},{97,65},{2,98}... | collective-permute-start | bytes 786440 | tf_op jit(solution)/shard_map/ppermute | solution.py:245
  54.9 13.3 %collective-permute-start.5 = (bf16[32,2,16,128]{3,2,1,0:T(8,128)(2,1)S(1)}, bf16[32,2,16,128]{3,2,1,0:T(8,128)(2,1)S(1)}, u32[]{:S(2)}, u32[]{:S(2)}) collective-permute-start(bf16[32,2,16,128]{3,2,1,0:T(8,128)(2,1)S(1)} %all-to-all-done.refs_0_), channel_id=1, source_target_pairs={{0,32},{32,64},{64,96},{96,0},{1,33},{33,65},{65,97},{97,1},{2,34}... | collective-permute-start | bytes 786440 | tf_op jit(solution)/shard_map/ppermute | solution.py:245
  54.9 20.1 %collective-permute-start.7 = (bf16[32,2,16,128]{3,2,1,0:T(8,128)(2,1)S(1)}, bf16[32,2,16,128]{3,2,1,0:T(8,128)(2,1)S(1)}, u32[]{:S(2)}, u32[]{:S(2)}) collective-permute-start(bf16[32,2,16,128]{3,2,1,0:T(8,128)(2,1)S(1)} %all-to-all-done.refs_0_), channel_id=1, source_target_pairs={{0,64},{32,96},{64,0},{96,32},{1,65},{33,97},{65,1},{97,33},{2,66}... | collective-permute-start | bytes 786440 | tf_op jit(solution)/shard_map/ppermute | solution.py:245
  67.9 13.2 %collective-permute-start.4 = (s16[16,72,128]{2,1,0:T(8,128)(2,1)S(1)}, s16[16,72,128]{2,1,0:T(8,128)(2,1)S(1)}, u32[]{:S(2)}, u32[]{:S(2)}) collective-permute-start(s16[16,72,128]{2,1,0:T(8,128)(2,1)S(1)} %attend.5), channel_id=1, source_target_pairs={{0,32},{32,64},{64,96},{96,0},{1,33},{33,65},{65,97},{97,1},{2,34}... | collective-permute-start | bytes 884744 | tf_op jit(solution)/shard_map/ppermute | solution.py:245
  70.7 10.4 %collective-permute-start.6 = (s16[16,72,128]{2,1,0:T(8,128)(2,1)S(1)}, s16[16,72,128]{2,1,0:T(8,128)(2,1)S(1)}, u32[]{:S(2)}, u32[]{:S(2)}) collective-permute-start(s16[16,72,128]{2,1,0:T(8,128)(2,1)S(1)} %attend.6), channel_id=1, source_target_pairs={{0,96},{32,0},{64,32},{96,64},{1,97},{33,1},{65,33},{97,65},{2,98}... | collective-permute-start | bytes 884744 | tf_op jit(solution)/shard_map/ppermute | solution.py:245
  77.4 8.7 %collective-permute-start.8 = (s16[16,72,128]{2,1,0:T(8,128)(2,1)S(1)}, s16[16,72,128]{2,1,0:T(8,128)(2,1)S(1)}, u32[]{:S(2)}, u32[]{:S(2)}) collective-permute-start(s16[16,72,128]{2,1,0:T(8,128)(2,1)S(1)} %attend.7), channel_id=1, source_target_pairs={{0,64},{32,96},{64,0},{96,32},{1,65},{33,97},{65,1},{97,33},{2,66}... | collective-permute-start | bytes 884744 | tf_op jit(solution)/shard_map/ppermute | solution.py:245
  104.1 8.6 %collective-permute-start.9 = (bf16[32,128]{1,0:T(8,128)(2,1)S(1)}, bf16[32,128]{1,0:T(8,128)(2,1)S(1)}, u32[]{:S(2)}, u32[]{:S(2)}) collective-permute-start(bf16[32,128]{1,0:T(8,128)(2,1)S(1)} %get-tuple-element.8), channel_id=1, source_target_pairs={{0,1},{1,0},{2,3},{3,2},{4,5},{5,4},{6,7},{7,6},{8,9},{9,8},{10,11... | collective-permute-start | bytes 24584 | tf_op jit(solution)/shard_map/ppermute | solution.py:307
